TPU v7x, 32 devices: a whole 2x2x4 slice. The times are simulated.
32 devices in a mesh: grp: 16 (over z, y, core), col: 2 (over x).
Axes of the slice: x: 2, y: 2, z: 4, core: 2. Of those that a mesh axis runs over, the one named last changes fastest.
Arguments:
- grad: float32 [4096, 16384], P('col', 'grp'), may hold values from -1.8 to 1.8
- exp_avg: float32 [4096, 16384], P('col', 'grp'), may hold values from -1.8 to 1.8
- exp_avg_sq: float32 [4096, 16384], P('col', 'grp'), may hold values from 0.01 to 0.36
- left_basis: bfloat16 [4096, 4096], P('grp', 'col'), may hold values from -1 to 1
- right_basis: bfloat16 [16384, 512], P('grp', 'col'), may hold values from -1 to 1
- gram_left: float32 [4096, 4096], P('grp', 'col'), may hold values from -6 to 6
- gram_right: float32 [16384, 512], P('grp', 'col'), may hold values from -6 to 6
Outputs:
- update: float32 [4096, 16384], P('col', 'grp')
- first_moment: float32 [4096, 16384], P('col', 'grp')
- second_moment: float32 [4096, 16384], P('col', 'grp')
- left_stat: float32 [4096, 4096], P('grp', 'col')
- right_stat: float32 [16384, 512], P('grp', 'col')
All inputs are finite; a program needn't handle non-finite values.
Results may differ from a plain program's by a relative error of at most 0.0041.
Values may be sent and summed in bfloat16 or wider, within the bound.
No kernel may reach another device: no remote copies, remote signals or barrier semaphores. Data moves between devices by JAX's collectives and lax.ppermute only.
A program may use at most 256 MiB of HBM per device.

v0:
```python
import jax
import jax.numpy as jnp
from jax import lax
from jax.sharding import PartitionSpec as P

RB = 512


decay = 0.95
bias_fix = 1.0 - decay**10


def local(grad, exp_avg, exp_avg_sq, left_basis, right_basis, gram_left, gram_right):
    col_count = lax.axis_size("col")
    rows_here, cols_here = grad.shape
    block_count = cols_here // RB
    rounded = grad.astype(jnp.bfloat16)
    panels = lax.all_gather(right_basis, "col", axis=1, tiled=True)
    blocks = panels.reshape(block_count, RB, RB)
    gathered = lax.all_gather(rounded, "col", axis=0, tiled=True)
    height = gathered.shape[0]
    product = jnp.einsum(
        "mbj,bjr->mbr",
        gathered.reshape(height, block_count, RB),
        blocks,
        preferred_element_type=jnp.float32,
    )
    turned = product.reshape(height, cols_here).astype(jnp.bfloat16)
    left_cols = lax.all_gather(left_basis, "grp", axis=0, tiled=True)
    rotated = lax.dot_general(
        left_cols, turned, (((0,), (0,)), ((), ())), preferred_element_type=jnp.float32
    )
    first_moment = decay * exp_avg + (1.0 - decay) * rotated
    second_moment = decay * exp_avg_sq + (1.0 - decay) * rotated * rotated
    direction = (first_moment / bias_fix / (jnp.sqrt(second_moment / bias_fix) + 1e-08)).astype(
        jnp.bfloat16
    )
    left_rows = lax.all_to_all(left_cols, "col", split_axis=0, concat_axis=1, tiled=True)
    back = jnp.dot(
        left_rows,
        lax.all_gather(direction, "col", axis=0, tiled=True),
        preferred_element_type=jnp.float32,
    )
    back = back.astype(jnp.bfloat16)
    update = jnp.einsum(
        "mbr,bjr->mbj",
        back.reshape(rows_here, block_count, RB),
        blocks,
        preferred_element_type=jnp.float32,
    )
    update = update.reshape(rows_here, cols_here)
    left_term = lax.psum_scatter(
        lax.dot_general(
            gathered, rounded, (((1,), (1,)), ((), ())), preferred_element_type=jnp.float32
        ),
        "grp",
        scatter_dimension=0,
        tiled=True,
    )
    left_stat = decay * gram_left + (1.0 - decay) * left_term
    share = RB // col_count
    offset = lax.axis_index("col") * share
    whole_blocks = gathered.reshape(gathered.shape[0], block_count, RB)
    narrow = lax.dynamic_slice_in_dim(whole_blocks, offset, share, 2)
    right_term = jnp.einsum(
        "mbj,mbr->bjr", whole_blocks, narrow, preferred_element_type=jnp.float32
    )
    right_stat = decay * gram_right + (1.0 - decay) * right_term.reshape(cols_here, share)
    return (update, first_moment, second_moment, left_stat, right_stat)


def solution(mesh):
    return jax.shard_map(
        local,
        mesh=mesh,
        in_specs=(
            P("col", "grp"),
            P("col", "grp"),
            P("col", "grp"),
            P("grp", "col"),
            P("grp", "col"),
            P("grp", "col"),
            P("grp", "col"),
        ),
        out_specs=(
            P("col", "grp"),
            P("col", "grp"),
            P("col", "grp"),
            P("grp", "col"),
            P("grp", "col"),
        ),
        check_vma=False,
    )
```

profile of v0, /device:TPU:0, one launch (start us, length us, event | category | flops | bytes accessed | tf_op | source)
XLA Modules:
  0.0 815.0 jit_solution(15229390837524339780)
XLA Ops:
  7.2 0.0 all-gather.5.cloned.1.call-start
  7.2 0.7 all-gather.5.cloned.1.call-update
  7.9 0.0 all-gather.7.cloned.1.call-start
  7.9 7.3 copy.32
  15.3 0.0 all-gather.7.cloned.1.call-update
  15.3 0.0 all-gather.9.cloned.1.call-start
  15.4 0.7 all-gather.9.cloned.1.call-update
  16.0 0.0 all-gather.11.cloned.1.call-start
  16.1 9.2 %copy.31 = f32[2048,1024]{0,1:T(8,128)} copy(f32[2048,1024]{1,0:T(8,128)} %param.8) | data formatting | bytes 16777216 | tf_op args[1]
  25.3 9.1 %copy.35 = f32[2048,1024]{0,1:T(8,128)} copy(f32[2048,1024]{1,0:T(8,128)} %param.9) | data formatting | bytes 16777216 | tf_op args[2]
  34.4 104.7 %all-gather.7.cloned.1.call-done = bf16[4096,1024]{0,1:T(8,128)(2,1)} async-done(((bf16[2048,1024]{0,1:T(8,128)(2,1)}), bf16[4096,1024]{0,1:T(8,128)(2,1)}) %all-gather.7.cloned.1.call-update) | async-done | bytes 8388624 | tf_op jit(solution)/shard_map/all_gather | solution.py:20
  139.1 12.1 %convolution_convert_fusion = bf16[2,512,4096]{2,1,0:T(8,128)(2,1)} fusion(bf16[2,512,512]{2,1,0:T(8,128)(2,1)} %bitcast.38, bf16[4096,2,512]{0,2,1:T(8,128)(2,1)} %bitcast.40), kind=kOutput, calls=%fused_computation.4 | convolution fusion | flops 4299161600 | bytes 17825792 | tf_op jit(solution)/shard_map/mbj,bjr->mbr/dot_general | solution.py:22
  151.2 116.5 %all-gather.9.cloned.1.call-done = bf16[4096,2048]{1,0:T(8,128)(2,1)} async-done(((bf16[256,2048]{1,0:T(8,128)(2,1)}), bf16[4096,2048]{1,0:T(8,128)(2,1)}) %all-gather.9.cloned.1.call-update) | async-done | bytes 16777232 | tf_op jit(solution)/shard_map/all_gather | solution.py:29
  267.7 33.8 %divide_convert_fusion = (bf16[2048,1024]{0,1:T(8,128)(2,1)}, f32[2048,1024]{0,1:T(8,128)}, f32[2048,1024]{0,1:T(8,128)}) fusion(f32[2048,1024]{0,1:T(8,128)} %copy.31, f32[2048,1024]{0,1:T(8,128)} %copy.35, bf16[4096,1024]{0,1:T(8,128)(2,1)} %bitcast.42, bf16[4096,2048]{1,0:T(8,128)(2,1)} %all-gather.9.cloned.1.call-done), kind=kOutput, calls=%fused_computation.3 | convolution fusion | flops 17202937856 | bytes 62914560 | tf_op jit(solution)/shard_map/dot_general | solution.py:30
  301.5 0.0 all-gather.11.cloned.1.call-update
  301.5 0.2 reduce-scatter.2.cloned.1.call-start
  301.7 25.6 %fusion.11 = f32[4096,2048]{1,0:T(8,128)} fusion(bf16[4096,1024]{0,1:T(8,128)(2,1)} %all-gather.7.cloned.1.call-done, bf16[2048,1024]{0,1:T(8,128)(2,1)} %copy.32), kind=kOutput, calls=%fused_computation.13 | convolution fusion | flops 17179869184 | bytes 46137344 | tf_op jit(solution)/shard_map/dot_general | solution.py:53
  327.3 0.0 reduce-scatter.2.cloned.1.call-update
  327.3 9.7 %all-to-all-start = ((bf16[2,2048,2048]{2,1,0:T(8,128)(2,1)}), bf16[2,2048,2048]{2,1,0:T(8,128)(2,1)}, u32[]{:S(2)}, u32[]{:S(2)}) async-start(bf16[2,2048,2048]{2,1,0:T(8,128)(2,1)} %bitcast.35), calls=%async_computation | async-start | bytes 33554432 | tf_op jit(solution)/shard_map/all_to_all | solution.py:38
  337.0 0.0 copy-start.2
  337.1 7.1 fusion.6
  344.2 0.3 copy.39
  344.5 1.1 bitcast_add_fusion
  345.6 9.2 %copy.41 = f32[2048,1024]{1,0:T(8,128)} copy(f32[2048,1024]{0,1:T(8,128)} %get-tuple-element.21) | data formatting | bytes 16777216
  354.9 9.2 %copy.42 = f32[2048,1024]{1,0:T(8,128)} copy(f32[2048,1024]{0,1:T(8,128)} %get-tuple-element.22) | data formatting | bytes 16777216
  364.1 219.3 %all-to-all-done = bf16[2,2048,2048]{2,1,0:T(8,128)(2,1)} async-done(((bf16[2,2048,2048]{2,1,0:T(8,128)(2,1)}), bf16[2,2048,2048]{2,1,0:T(8,128)(2,1)}, u32[]{:S(2)}, u32[]{:S(2)}) %all-to-all-start) | async-done | bytes 16777248 | tf_op jit(solution)/shard_map/all_to_all | solution.py:38
  583.4 22.8 %copy.36 = bf16[2048,2,2048]{0,2,1:T(8,128)(2,1)} copy(bf16[2048,2,2048]{2,0,1:T(8,128)(2,1)} %bitcast.6) | data formatting | bytes 33554432 | tf_op jit(solution)/shard_map/all_to_all | solution.py:38
  606.2 22.8 %convolution_convert_fusion.1 = bf16[1024,2048]{1,0:T(8,128)(2,1)S(1)} fusion(bf16[4096,1024]{0,1:T(8,128)(2,1)} %all-gather.11.cloned.1.call-done, bf16[2048,4096]{0,1:T(8,128)(2,1)} %bitcast.36), kind=kOutput, calls=%fused_computation.7 | convolution fusion | flops 17181966336 | bytes 29360128 | tf_op jit(solution)/shard_map/dot_general | solution.py:39
  629.0 5.6 fusion.12
  634.6 9.4 %copy.40 = f32[2048,1024]{1,0:T(8,128)} copy(f32[2048,1024]{0,1:T(8,128)} %bitcast.34) | data formatting | bytes 16777216
  644.0 161.2 %reduce-scatter.2.cloned.1.call-done = f32[256,2048]{1,0:T(8,128)} async-done(((f32[4096,2048]{1,0:T(8,128)}), f32[256,2048]{1,0:T(8,128)}) %reduce-scatter.2.cloned.1.call-update) | async-done | bytes 2097168 | tf_op jit(solution)/shard_map/reduce_scatter | solution.py:52
  805.2 3.3 multiply_add_fusion.1
  (7 shorter events, 0.0 us)
Async XLA Ops:
  7.2 27.2 %all-gather.5.cloned.1.call-start = ((), (), s32[]{:S(2)}) async-start(), calls=%async_computation.2 | async-start | bytes 1572864 | tf_op jit(solution)/shard_map/all_gather | solution.py:18
  7.9 131.2 %all-gather.7.cloned.1.call-start = ((), (), s32[]{:S(2)}) async-start(), calls=%async_computation.3 | async-start | bytes 12582912 | tf_op jit(solution)/shard_map/all_gather | solution.py:20
  15.3 252.4 %all-gather.9.cloned.1.call-start = ((), (), s32[]{:S(2)}) async-start(), calls=%async_computation.4 | async-start | bytes 17825792 | tf_op jit(solution)/shard_map/all_gather | solution.py:29
  16.0 590.2 %all-gather.11.cloned.1.call-start = ((), (), s32[]{:S(2)}) async-start(), calls=%async_computation.5 | async-start | bytes 12582912 | tf_op jit(solution)/shard_map/all_gather | solution.py:41
  301.5 503.7 %reduce-scatter.2.cloned.1.call-start = ((), (), s32[]{:S(2)}) async-start(), calls=%async_computation.6 | async-start | bytes 35651584 | tf_op jit(solution)/shard_map/reduce_scatter | solution.py:52
  327.3 256.1 %all-to-all-start = ((bf16[2,2048,2048]{2,1,0:T(8,128)(2,1)}), bf16[2,2048,2048]{2,1,0:T(8,128)(2,1)}, u32[]{:S(2)}, u32[]{:S(2)}) async-start(bf16[2,2048,2048]{2,1,0:T(8,128)(2,1)} %bitcast.35), calls=%async_computation | async-start | bytes 33554432 | tf_op jit(solution)/shard_map/all_to_all | solution.py:38
  337.0 7.5 copy-start.2
  606.2 22.8 %copy-start = (bf16[1024,512]{1,0:T(8,128)(2,1)S(1)}, bf16[1024,512]{1,0:T(8,128)(2,1)}, u32[]{:S(2)}) copy-start(bf16[1024,512]{1,0:T(8,128)(2,1)} %all-gather.5.cloned.1.call-done) | copy-start | bytes 3145732
  634.6 170.6 %copy-start.1 = (f32[256,2048]{1,0:T(8,128)S(1)}, f32[256,2048]{1,0:T(8,128)}, u32[]{:S(2)}) copy-start(f32[256,2048]{1,0:T(8,128)} %param.12) | copy-start | bytes 6291460
Sparse Core Ops, SparseCore 0:
  9.5 23.9 all-gather.4
  35.0 103.9 all-gather.6
  141.2 126.4 all-gather.8
  301.6 165.6 all-gather.10
  471.4 333.7 reduce-scatter.1
where the time goes:
time: 816 us; the launch traced here: 815 us
  waiting for transfers between devices  603 us (74%)
  matrix products  107 us (13%)
  local copies, waits for them, and re-layouts  76.7 us (9%)
  between operations  13.8 us (2%)
  starting transfers between devices  10.1 us (1%)
    all_to_all x1, waiting for transfers between devices, local(): lax.all_to_all(left_cols, 'col', split_axis=0, concat_axis=1, tiled=True)  219 us
    reduce_scatter x1, waiting for transfers between devices, local(): lax.psum_scatter(lax.dot_general(gathered, rounded, (((1,), (1,)), ((), (...  161 us
    all_gather x1, waiting for transfers between devices, local(): left_cols = lax.all_gather(left_basis, 'grp', axis=0, tiled=True)  117 us
    all_gather x1, waiting for transfers between devices, local(): gathered = lax.all_gather(rounded, 'col', axis=0, tiled=True)  105 us
    unnamed x12, local copies, waits for them, and re-layouts  53.5 us
    dot_general x1, matrix products, local(): lax.dot_general(left_cols, turned, (((0,), (0,)), ((), ())), preferred_el...  33.8 us
    dot_general x1, matrix products, local(): lax.dot_general(gathered, rounded, (((1,), (1,)), ((), ())), preferred_el...  25.6 us
    all_to_all x1, local copies, waits for them, and re-layouts, local(): lax.all_to_all(left_cols, 'col', split_axis=0, concat_axis=1, tiled=True)  22.8 us
  transfers between devices with their start and end apart: 6, of which 4 were waited for; matrix products, arithmetic and copies ran while one was open for 19% of the time, Pallas kernels for 0%

commit v1 on v0

v1 whole, which is shorter than its diff:
```python
import functools

import jax
import jax.numpy as jnp
from jax import lax
from jax.experimental import pallas as pl
from jax.experimental.pallas import tpu as pltpu
from jax.sharding import PartitionSpec as P


RB = 512

decay = 0.95
bias_fix = 1.0 - decay**10

F32 = jnp.float32
BF16 = jnp.bfloat16
ANY = pl.BlockSpec(memory_space=pl.ANY)


def params(grid_rank=1):
    return pltpu.CompilerParams(
        dimension_semantics=("arbitrary",) * grid_rank, vmem_limit_bytes=58 * 2**20
    )


def cost(flops, moved):
    return pl.CostEstimate(flops=flops, bytes_accessed=moved, transcendentals=0)


def dot(a, b, ca, cb):
    return lax.dot_general(a, b, (((ca,), (cb,)), ((), ())), preferred_element_type=F32)


def scalars(*values):
    return jnp.stack([jnp.asarray(v, jnp.int32) for v in values])


def blank(shape, kind):
    return pl.pallas_call(
        lambda out: None, out_shape=jax.ShapeDtypeStruct(shape, kind), out_specs=ANY, name="blank"
    )()


def block_kernel(pieces, sections, fill, turn, strips, s_ref, at_ref, *refs):
    lefts, refs = refs[:pieces], refs[pieces:]
    right, refs = refs[0], refs[1:]
    grads, refs = refs[:sections], refs[sections:]
    avg, avg_sq = refs[:2]
    first_out, second_out, other_out, own_out, left, turned, direction, sems = refs[-8:]
    part, tile = grads[0].shape[0], avg.shape[0]
    strip = own_out.shape[0]
    step = pl.program_id(0)
    lead = sections * fill

    def load(c):
        lanes = pl.ds(c * tile, tile)
        for k in range(pieces):
            rows = lefts[k].shape[0]
            base = pl.multiple_of(at_ref[k], 16)
            pltpu.make_async_copy(lefts[k].at[:, lanes], left.at[pl.ds(base, rows), lanes], sems.at[c]).start()

    for c in range(turn):

        @pl.when(step == min(c, lead - 1))
        def _(c=c):
            load(c)

    for k in range(sections):

        @pl.when((step >= k * fill) & (step < (k + 1) * fill))
        def _(k=k):
            base = pl.multiple_of((s_ref[k] * fill + step - k * fill) * part, part)
            turned[pl.ds(base, part), :] = dot(grads[k][...], right[...], 1, 0).astype(BF16)

    for c in range(turn):

        @pl.when(step == lead + c)
        def _(c=c):
            lanes = pl.ds(c * tile, tile)
            pltpu.make_async_copy(left.at[:, lanes], left.at[:, lanes], sems.at[c]).wait()
            rotated = dot(left[:, lanes], turned[...], 0, 0)
            first = decay * avg[...] + (1.0 - decay) * rotated
            second = decay * avg_sq[...] + (1.0 - decay) * rotated * rotated
            first_out[...] = first
            second_out[...] = second
            direction[lanes, :] = (
                first / bias_fix / (jnp.sqrt(second / bias_fix) + 1e-08)
            ).astype(BF16)

    spin = step - lead - turn
    split = (sections - 1) * strips

    @pl.when(spin >= 0)
    def _():
        section = s_ref[lax.rem(spin // strips + 1, sections)]
        base = pl.multiple_of((section * strips + lax.rem(spin, strips)) * strip, strip)
        share = dot(left[pl.ds(base, strip), :], direction[...], 1, 0)

        @pl.when(spin < split)
        def _():
            other_out[...] = share.astype(BF16)

        @pl.when(spin >= split)
        def _():
            own_out[...] = share


def block(b, order, left, right, grads, avg, avg_sq, old, after=()):
    places, lefts = left
    pieces = len(lefts)
    width = lefts[0].shape[1]
    rows, cols = avg.shape
    sections = len(grads)
    height = sections * rows
    part, tile, strip = min(512, rows), min(512, rows), min(512, rows)
    fill, turn, strips = rows // part, rows // tile, rows // strip
    lead = sections * fill
    split = max(sections - 1, 1) * strips

    def column(i, s, a):
        return (jnp.clip(i - lead, 0, turn - 1), b)

    def part_of(k):
        return lambda i, s, a: (jnp.clip(i - k * fill, 0, fill - 1), 0)

    in_specs = [
        *[ANY] * pieces,
        pl.BlockSpec((RB, RB), lambda i, s, a: (b, 0)),
        *[pl.BlockSpec((part, RB), part_of(k)) for k in range(sections)],
        pl.BlockSpec((tile, RB), column),
        pl.BlockSpec((tile, RB), column),
    ]
    args = [order, places, *lefts, right, *grads, avg, avg_sq]
    aliases = {}
    if old is not None:
        in_specs += [ANY, ANY]
        aliases = {len(args): 0, len(args) + 1: 1}
        args += list(old)
    in_specs += [ANY] * len(after)
    args += list(after)
    return pl.pallas_call(
        functools.partial(block_kernel, pieces, sections, fill, turn, strips),
        grid_spec=pltpu.PrefetchScalarGridSpec(
            num_scalar_prefetch=2,
            grid=(lead + turn + sections * strips,),
            in_specs=in_specs,
            out_specs=[
                pl.BlockSpec((tile, RB), column),
                pl.BlockSpec((tile, RB), column),
                pl.BlockSpec((strip, RB), lambda i, s, a: (jnp.clip(i - lead - turn, 0, split - 1), 0)),
                pl.BlockSpec(
                    (strip, RB), lambda i, s, a: (jnp.clip(i - lead - turn - split, 0, strips - 1), 0)
                ),
            ],
            scratch_shapes=[
                pltpu.VMEM((height, width), BF16),
                pltpu.VMEM((height, RB), BF16),
                pltpu.VMEM((rows, RB), BF16),
                pltpu.SemaphoreType.DMA((turn,)),
            ],
        ),
        out_shape=[
            jax.ShapeDtypeStruct((rows, cols), F32),
            jax.ShapeDtypeStruct((rows, cols), F32),
            jax.ShapeDtypeStruct((split * strip, RB), BF16),
            jax.ShapeDtypeStruct((rows, RB), F32),
        ],
        input_output_aliases=aliases,
        compiler_params=params(),
        cost_estimate=cost(4 * height * RB * (rows + RB), 2 * height * (width + RB) + 24 * rows * RB),
        name="block",
    )(*args)


def update_kernel(count, own, right, *refs):
    total = own[...]
    for part in refs[:count]:
        total = total + part[...].astype(F32)
    refs[-1][...] = dot(total.astype(BF16), right[...], 1, 1)


def update_block(b, own, parts, right, cols, old, after=()):
    rows = own.shape[0]
    tile = min(512, rows)
    row = lambda i: (i, 0)
    in_specs = [
        pl.BlockSpec((tile, RB), row),
        pl.BlockSpec((RB, RB), lambda i: (b, 0)),
        *[pl.BlockSpec((tile, RB), row)] * len(parts),
    ]
    args = [own, right, *parts]
    aliases = {}
    if old is not None:
        in_specs.append(ANY)
        aliases = {len(args): 0}
        args.append(old)
    in_specs += [ANY] * len(after)
    args += list(after)
    return pl.pallas_call(
        functools.partial(update_kernel, len(parts)),
        grid=(rows // tile,),
        in_specs=in_specs,
        out_specs=pl.BlockSpec((tile, RB), lambda i: (i, b)),
        out_shape=jax.ShapeDtypeStruct((rows, cols), F32),
        input_output_aliases=aliases,
        compiler_params=params(),
        cost_estimate=cost(2 * rows * RB * RB, rows * RB * 10),
        name="update",
    )(*args)


def gram_kernel(pieces, s_ref, *refs):
    total = None
    for k in range(pieces):
        term = dot(refs[k][...], refs[pieces + k][...], 1, 1)
        total = term if total is None else total + term
    refs[-1][0] = total.astype(BF16)


def left_gram(section, core, slab, count, tops, sides, old, after=()):
    rows, width = tops[0].shape
    pieces = len(tops)
    steps = rows // (2 * slab)
    in_specs = [
        *[pl.BlockSpec((slab, width), lambda i, s: (2 * i + s[1], 0))] * pieces,
        *[pl.BlockSpec((rows, width), lambda i, s: (0, 0))] * pieces,
    ]
    args = [scalars(section, core), *tops, *sides]
    aliases = {}
    if old is not None:
        in_specs.append(ANY)
        aliases = {len(args): 0}
        args.append(old)
    in_specs += [ANY] * len(after)
    args += list(after)
    return pl.pallas_call(
        functools.partial(gram_kernel, pieces),
        grid_spec=pltpu.PrefetchScalarGridSpec(
            num_scalar_prefetch=1,
            grid=(steps,),
            in_specs=in_specs,
            out_specs=pl.BlockSpec((1, slab, rows), lambda i, s: (s[0] * steps + i, 0, 0)),
        ),
        out_shape=jax.ShapeDtypeStruct((count, slab, rows), BF16),
        input_output_aliases=aliases,
        compiler_params=params(),
        cost_estimate=cost(rows * rows * width * pieces, rows * width * 3 * pieces + 2 * rows * rows),
        name="left_gram",
    )(*args)


def right_kernel(sections, s_ref, gram, *refs):
    out, total = refs[-2:]
    step = pl.program_id(0)

    @pl.when(step == 0)
    def _():
        total[...] = jnp.zeros_like(total)

    for k in range(sections):
        total[...] += dot(refs[2 * k][...], refs[2 * k + 1][...], 0, 0)

    @pl.when(step == pl.num_programs(0) - 1)
    def _():
        out[...] = decay * gram[...] + (1.0 - decay) * total[...]


def right_stat_block(b, place, gram, grads, old, after=()):
    rows = grads[0].shape[0]
    share = gram.shape[1]
    tile = min(512, rows)
    in_specs = [pl.BlockSpec((RB, share), lambda i, s: (b, 0))]
    args = [scalars(place), gram]
    lanes = share % 128 == 0
    for g in grads:
        in_specs += [
            pl.BlockSpec((tile, RB), lambda i, s: (i, 0)),
            pl.BlockSpec((tile, share), (lambda i, s: (i, s[0])) if lanes else (lambda i, s: (i, 0))),
        ]
        args += [g, g if lanes else lax.dynamic_slice_in_dim(g, place * share, share, 1)]
    aliases = {}
    if old is not None:
        in_specs.append(ANY)
        aliases = {len(args): 0}
        args.append(old)
    in_specs += [ANY] * len(after)
    args += list(after)
    return pl.pallas_call(
        functools.partial(right_kernel, len(grads)),
        grid_spec=pltpu.PrefetchScalarGridSpec(
            num_scalar_prefetch=1,
            grid=(rows // tile,),
            in_specs=in_specs,
            out_specs=pl.BlockSpec((RB, share), lambda i, s: (b, 0)),
            scratch_shapes=[pltpu.VMEM((RB, share), F32)],
        ),
        out_shape=jax.ShapeDtypeStruct(gram.shape, F32),
        input_output_aliases=aliases,
        compiler_params=params(),
        cost_estimate=cost(2 * rows * len(grads) * RB * share, rows * len(grads) * RB * 4),
        name="right_stat",
    )(*args)


class Places:
    def __init__(self):
        self.count = lax.axis_size("grp")
        self.outer = self.count // 4
        index = lax.axis_index("grp")
        self.z, self.y, self.core = index // 4, (index // 2) % 2, index % 2

    def send(self, x, dz=0, dy=0, dcore=0):
        pairs = []
        for i in range(self.count):
            z, y, core = i // 4, (i // 2) % 2, i % 2
            pairs.append((i, ((z + dz) % self.outer) * 4 + (y ^ dy) * 2 + (core ^ dcore)))
        return lax.ppermute(x, "grp", pairs)

    def pass_on(self, x, dz=0, dy=0, only=0):
        pairs = []
        for i in range(self.count):
            z, y, core = i // 4, (i // 2) % 2, i % 2
            if 0 <= z + only < self.outer:
                pairs.append((i, (z + dz) * 4 + (y ^ dy) * 2 + core))
        return lax.ppermute(x, "grp", pairs)

    def chip(self, dz, dy):
        return ((self.z + dz) % self.outer) * 2 + (self.y ^ dy)


def thirds(rows):
    a = rows // 16 // 3 * 16
    a = max(a, 16)
    return [(0, rows - 2 * a), (rows - 2 * a, a), (rows - a, a)]


def gather_left(at, left_basis):
    slab = left_basis.shape[0]
    far = at.outer // 2
    rows, pieces = [], []

    def send(x, **how):
        return at.send(x, **how)

    def put(x, dz, dy, start=0):
        for piece, core in ((x, at.core), (send(x, dcore=1), 1 - at.core)):
            rows.append((at.chip(dz, dy) * 2 + core) * slab + start)
            pieces.append(piece)

    got = {(0, 0): left_basis}
    got[0, 1] = send(left_basis, dy=1)
    for d in range(1, far + 1):
        got[d, 0] = send(got[d - 1, 0], dz=-1)
        if d < far:
            got[-d, 0] = send(got[1 - d, 0], dz=1)
            got[-d, 1] = send(got[1 - d, 1], dz=1)
            got[d, 1] = send(got[d, 0], dy=1)
    for key, x in got.items():
        put(x, *key)
    cut = thirds(slab)
    sources = ((got[far, 0], dict(dy=1)), (got[1 - far, 1], dict(dz=1)), (got[far - 1, 1], dict(dz=-1)))
    for (start, size), (source, how) in zip(cut, sources, strict=True):
        put(send(source[start : start + size], **how), far, 1, start)
    return scalars(*rows), pieces


class Reduction:
    def __init__(self, at, parts):
        self.at, self.parts = at, parts
        self.offsets = [dz for t in range(at.outer - 1, 0, -1) for dz in (t, -t)] + [0]
        self.came = {}
        for dz in self.offsets:
            self.came[dz] = [at.pass_on(self.part(dz, 1), dy=1, only=dz)]

    def part(self, dz, dy):
        return lax.dynamic_index_in_dim(self.parts, self.at.chip(dz, dy), 0, keepdims=False)

    def total(self, dz):
        total = self.part(dz, 0).astype(F32)
        for x in self.came[dz]:
            total = total + x.astype(F32)
        return total

    def round(self, t, after):
        self.parts, _ = lax.optimization_barrier((self.parts, after))
        sent = []
        for dz, way in ((t, 1), (-t, -1)):
            sent.append(self.total(dz).astype(BF16))
            self.came[dz - way].append(self.at.pass_on(sent[-1], dz=way, only=dz))
        return tuple(sent)


def step(grad, exp_avg, exp_avg_sq, left_basis, right_basis, gram_left, gram_right):
    at = Places()
    col_count = lax.axis_size("col")
    mine = lax.axis_index("col")
    rows_here, cols_here = grad.shape
    blocks = range(cols_here // RB)
    others = range(1, col_count)
    slab = gram_left.shape[0]

    def from_right(x, s):
        return lax.ppermute(x, "col", [((i + s) % col_count, i) for i in range(col_count)])

    def to_right(x, s):
        return lax.ppermute(x, "col", [(i, (i + s) % col_count) for i in range(col_count)])

    def twin(x):
        return at.send(x, dcore=1)

    shares = [right_basis] + [from_right(right_basis, s) for s in others]
    own = [grad[:, b * RB : (b + 1) * RB].astype(BF16) for b in blocks]
    grads = [[own[b]] + [from_right(own[b], s) for s in others] for b in blocks]
    sections = [(mine + s) % col_count for s in range(col_count)]
    share = right_basis.shape[1]
    right = blank((cols_here, RB), BF16)
    for s in range(col_count):
        right = lax.dynamic_update_slice(right, shares[s], (0, sections[s] * share))
    order = scalars(*sections)

    left = gather_left(at, left_basis)

    twins = [[twin(x) for x in grads[b]] for b in blocks]
    sides = [grads[b][0] for b in blocks] + [twins[b][0] for b in blocks]
    parts = moments = update = right_stat = None
    kept, came, after = [], [], ()
    for s in range(col_count):
        tops = [grads[k][s] for k in blocks] + [twins[k][s] for k in blocks]
        parts = left_gram(sections[s], at.core, slab, at.count // 2, tops, sides, parts)
    sums = Reduction(at, parts)
    rounds = list(range(at.outer - 1, 0, -1))
    after = (parts,)
    for b in blocks:
        first, second, shared, share = block(
            b, order, left, right, grads[b], exp_avg, exp_avg_sq, moments, after
        )
        moments = (first, second)
        kept.append(share)
        came.append([to_right(shared[(s - 1) * rows_here : s * rows_here], s) for s in others])
        after = sums.round(rounds.pop(0), share) if rounds else (share,)
    for b in blocks:
        right_stat = right_stat_block(b, mine, gram_right, grads[b], right_stat, after)
    for b in blocks[:-1]:
        update = update_block(b, kept[b], came[b], right, cols_here, update, after)
    while rounds:
        after = sums.round(rounds.pop(0), right_stat)
    left_stat = decay * gram_left + (1.0 - decay) * sums.total(0)
    update = update_block(blocks[-1], kept[-1], came[-1], right, cols_here, update, after)
    return (update, *moments, left_stat, right_stat)


def solution(mesh):
    return jax.shard_map(
        step,
        mesh=mesh,
        in_specs=(
            P("col", "grp"),
            P("col", "grp"),
            P("col", "grp"),
            P("grp", "col"),
            P("grp", "col"),
            P("grp", "col"),
            P("grp", "col"),
        ),
        out_specs=(
            P("col", "grp"),
            P("col", "grp"),
            P("col", "grp"),
            P("grp", "col"),
            P("grp", "col"),
        ),
        check_vma=False,
    )
```

time: 816 us -> 432 us (0.53)
  the two profiles are of different devices: /device:TPU:0 before, /device:TPU:24 now
where the time goes in v1:
time: 432 us; the launch traced here: 425 us
  waiting for transfers between devices  210 us (49%)
  Pallas kernels  128 us (30%)
  starting transfers between devices  49.5 us (11%)
  other arithmetic  22.4 us (5%)
  local copies, waits for them, and re-layouts  13.6 us (3%)
    pallas_call x2, Pallas kernels, block(): pl.pallas_call(functools.partial(block_kernel, pieces, sections, fill, tu...  74.6 us
    ppermute x23, waiting for transfers between devices, send(): return lax.ppermute(x, 'grp', pairs)  63.4 us
    ppermute x3, waiting for transfers between devices, from_right(): lax.ppermute(x, 'col', [((i + s) % col_count, i) for i in range(col_count)])  62.3 us
    ppermute x2, waiting for transfers between devices, to_right(): lax.ppermute(x, 'col', [(i, (i + s) % col_count) for i in range(col_count)])  55.9 us
    pallas_call x2, Pallas kernels, left_gram(): pl.pallas_call(functools.partial(gram_kernel, pieces), grid_spec=pltpu.Pr...  30.6 us
    ppermute x13, starting transfers between devices, pass_on(): return lax.ppermute(x, 'grp', pairs)  29.1 us
    ppermute x13, waiting for transfers between devices, pass_on(): return lax.ppermute(x, 'grp', pairs)  28.4 us
    ppermute x23, starting transfers between devices, send(): return lax.ppermute(x, 'grp', pairs)  14.7 us
  transfers between devices with their start and end apart: 41, of which 8 were waited for; matrix products, arithmetic and copies ran while one was open for 7% of the time, Pallas kernels for 30%

profile of v1, /device:TPU:24, one launch (start us, length us, event | category | flops | bytes accessed | tf_op | source)
XLA Modules:
  0.0 425.2 jit_solution(16145167518236006137)
XLA Ops:
  0.7 2.0 collective-permute-start.3
  5.7 4.0 convert.11
  9.8 38.5 %collective-permute-done.5.refs_6_ = bf16[256,2048]{1,0:T(8,128)(2,1)S(1)} collective-permute-done((bf16[256,2048]{1,0:T(8,128)(2,1)}, bf16[256,2048]{1,0:T(8,128)(2,1)S(1)}, u32[]{:S(2)}, u32[]{:S(2)}) %collective-permute-start.5) | collective-permute-done | bytes 1048608 | tf_op jit(solution)/shard_map/ppermute | solution.py:318
  54.0 24.9 %collective-permute-done.11.refs_12_ = bf16[256,2048]{1,0:T(8,128)(2,1)} collective-permute-done((bf16[256,2048]{1,0:T(8,128)(2,1)S(1)}, bf16[256,2048]{1,0:T(8,128)(2,1)}, u32[]{:S(2)}, u32[]{:S(2)}) %collective-permute-start.11) | collective-permute-done | bytes 1048608 | tf_op jit(solution)/shard_map/ppermute | solution.py:318
  80.7 17.9 %collective-permute-done.21.refs_0_.refs_22_.refs_2_.refs_3_ = bf16[2048,512]{1,0:T(8,128)(2,1)} collective-permute-done((bf16[2048,512]{1,0:T(8,128)(2,1)S(1)}, bf16[2048,512]{1,0:T(8,128)(2,1)}, u32[]{:S(2)}, u32[]{:S(2)}) %collective-permute-start.21) | collective-permute-done | bytes 2097184 | tf_op jit(solution)/shard_map/ppermute | solution.py:404
  98.6 44.4 %collective-permute-done.20.refs_1_.refs_22_.refs_2_.refs_3_ = bf16[2048,512]{1,0:T(8,128)(2,1)} collective-permute-done((bf16[2048,512]{1,0:T(8,128)(2,1)}, bf16[2048,512]{1,0:T(8,128)(2,1)}, u32[]{:S(2)}, u32[]{:S(2)}) %collective-permute-start.20) | collective-permute-done | bytes 2097184 | tf_op jit(solution)/shard_map/ppermute | solution.py:404
  150.3 3.4 collective-permute-start.15
  153.7 15.3 %left_gram.2.refs_8_ = bf16[8,256,2048]{2,1,0:T(8,128)(2,1)} custom-call(s32[2]{0:T(128)} %pad_add_fusion.2.s_ref, bf16[2048,512]{1,0:T(8,128)(2,1)} %copy-done, bf16[2048,512]{1,0:T(8,128)(2,1)} %get-tuple-element.41.refs_1_.refs_5_.refs_21_.refs_0_, bf16[2048,512]{1,0:T(8,128)(2,1)} %collective-permute-done.24.refs_2_.refs_6_, ...), custom_call_target="tpu_custom_call" | custom-call | flops 8589934592 | bytes 20971520 | tf_op jit(solution)/shard_map/left_gram/pallas_call | solution.py:237
  172.6 15.3 %left_gram.3.refs_25_ = bf16[8,256,2048]{2,1,0:T(8,128)(2,1)} custom-call(s32[2]{0:T(128)} %pad_add_fusion.1.s_ref, bf16[2048,512]{1,0:T(8,128)(2,1)} %collective-permute-done.21.refs_0_.refs_22_.refs_2_.refs_3_, bf16[2048,512]{1,0:T(8,128)(2,1)} %collective-permute-done.20.refs_1_.refs_22_.refs_2_.refs_3_, ...), custom_call_target="tpu_custom_call", output_to_operand_aliasing={{}: (9, {})} | custom-call | flops 8589934592 | bytes 20971520 | tf_op jit(solution)/shard_map/left_gram/pallas_call | solution.py:237
  189.3 5.7 %dynamic-slice_bitcast_fusion = (bf16[256,2048]{1,0:T(8,128)(2,1)S(1)}, bf16[256,2048]{1,0:T(8,128)(2,1)S(1)}, bf16[256,2048]{1,0:T(8,128)(2,1)}, bf16[256,2048]...) fusion(bf16[8,256,2048]{2,1,0:T(8,128)(2,1)} %left_gram.3.refs_25, ...), kind=kLoop, calls=%fused_computation.21 | loop fusion | bytes 14680092 | tf_op jit(solution)/shard_map/jit(dynamic_index_in_dim)/squeeze | solution.py:377
  195.0 2.4 collective-permute-start.36
  197.5 3.4 collective-permute-start.32
  202.5 2.4 collective-permute-start.27
  205.0 2.1 collective-permute-start.26
  207.1 37.3 %block.2 = (f32[2048,1024]{1,0:T(8,128)}, f32[2048,1024]{1,0:T(8,128)}, bf16[2048,512]{1,0:T(8,128)(2,1)}, f32[2048,512]{1,0:T(8,128)}) custom-call(s32[2]{0:T(128)} %pad_add_fusion.s_ref, s32[20]{0:T(128)} %stack.111.at_ref, bf16[256,2048]{1,0:T(8,128)(2,1)} %refs_0_.3, bf16[256,2048]{1,0:T(8,128)(2,1)} %copy-done.10, ...), custom_call_target="tpu_custom_call" | custom-call | flops 21474836480 | bytes 46137344 | tf_op jit(solution)/shard_map/block/pallas_call | solution.py:142
  244.4 22.7 %collective-permute-done.27 = bf16[256,2048]{1,0:T(8,128)(2,1)} collective-permute-done((bf16[256,2048]{1,0:T(8,128)(2,1)}, bf16[256,2048]{1,0:T(8,128)(2,1)}, u32[]{:S(2)}, u32[]{:S(2)}) %collective-permute-start.27) | collective-permute-done | bytes 1048608 | tf_op jit(solution)/shard_map/ppermute | solution.py:326
  267.1 4.1 fusion.12
  271.2 2.3 collective-permute-start.33
  275.3 37.3 %block.3 = (f32[2048,1024]{1,0:T(8,128)}, f32[2048,1024]{1,0:T(8,128)}, bf16[2048,512]{1,0:T(8,128)(2,1)}, f32[2048,512]{1,0:T(8,128)}) custom-call(s32[2]{0:T(128)} %pad_add_fusion.s_ref, s32[20]{0:T(128)} %stack.111.at_ref, bf16[256,2048]{1,0:T(8,128)(2,1)} %refs_0_.3, ...), custom_call_target="tpu_custom_call", output_to_operand_aliasing={{0}: (27, {}), {1}: (28, {})} | custom-call | flops 21474836480 | bytes 46137344 | tf_op jit(solution)/shard_map/block/pallas_call | solution.py:142
  314.2 4.0 fusion.9
  318.3 2.3 collective-permute-start.37
  320.6 1.8 collective-permute-start.35
  324.5 5.5 %right_stat.2.refs_4_ = f32[1024,256]{1,0:T(8,128)} custom-call(s32[1]{0:T(128)} %bitcast.31.s_ref, f32[1024,256]{1,0:T(8,128)} %gram.3, bf16[2048,512]{1,0:T(8,128)(2,1)} %copy-done, bf16[2048,512]{1,0:T(8,128)(2,1)} %copy-done, bf16[2048,512]{1,0:T(8,128)(2,1)} %collective-permute-done.21.refs_0_.refs_22_.refs_2_.refs_3_, ...), custom_call_target="tpu_custom_call" | custom-call | flops 1073741824 | bytes 8388608 | tf_op jit(solution)/shard_map/right_stat/pallas_call | solution.py:289
  330.0 5.5 %right_stat.3 = f32[1024,256]{1,0:T(8,128)} custom-call(s32[1]{0:T(128)} %bitcast.31.s_ref, f32[1024,256]{1,0:T(8,128)} %gram.3, bf16[2048,512]{1,0:T(8,128)(2,1)} %get-tuple-element.41.refs_1_.refs_5_.refs_21_.refs_0_, bf16[2048,512]{1,0:T(8,128)(2,1)} %get-tuple-element.41.refs_1_.refs_5_.refs_21_.refs_0_, ...), custom_call_target="tpu_custom_call", output_to_operand_aliasing={{}: (6, {})} | custom-call | flops 1073741824 | bytes 8388608 | tf_op jit(solution)/shard_map/right_stat/pallas_call | solution.py:289
  336.0 5.7 %collective-permute-done.37 = bf16[256,2048]{1,0:T(8,128)(2,1)} collective-permute-done((bf16[256,2048]{1,0:T(8,128)(2,1)S(1)}, bf16[256,2048]{1,0:T(8,128)(2,1)}, u32[]{:S(2)}, u32[]{:S(2)}) %collective-permute-start.37) | collective-permute-done | bytes 1048608 | tf_op jit(solution)/shard_map/ppermute | solution.py:326
  341.7 4.0 fusion.5
  345.8 5.5 %collective-permute-start.40 = (bf16[256,2048]{1,0:T(8,128)(2,1)S(1)}, bf16[256,2048]{1,0:T(8,128)(2,1)}, u32[]{:S(2)}, u32[]{:S(2)}) collective-permute-start(bf16[256,2048]{1,0:T(8,128)(2,1)S(1)} %get-tuple-element.34.refs_3_), channel_id=1, source_target_pairs={{8,0},{10,2},{12,4},{14,6},{16,8},{18,10},{20,12},{22,14},{24,16},... | collective-permute-start | bytes 3145736 | tf_op jit(solution)/shard_map/ppermute | solution.py:326
  352.5 18.8 %collective-permute-done.29.refs_0_ = bf16[2048,512]{1,0:T(8,128)(2,1)} collective-permute-done((bf16[2048,512]{1,0:T(8,128)(2,1)}, bf16[2048,512]{1,0:T(8,128)(2,1)}, u32[]{:S(2)}, u32[]{:S(2)}) %collective-permute-start.29) | collective-permute-done | bytes 2097184 | tf_op jit(solution)/shard_map/ppermute | solution.py:407
  371.3 6.1 %update.2.refs_1_ = f32[2048,1024]{1,0:T(8,128)} custom-call(f32[2048,512]{1,0:T(8,128)} %get-tuple-element.18.own, bf16[1024,512]{1,0:T(8,128)(2,1)} %constant_dynamic-update-slice_fusion.refs_20_.right, bf16[2048,512]{1,0:T(8,128)(2,1)} %collective-permute-done.29.refs_0_, bf16[256,2048]{1,0:T(8,128)(2,1)} %copy-done.2, bf16[256,2048]{1,0:T(8,128)(2,1)} %copy-done.1), custom_call_target="tpu_custom_call" | custom-call | flops 1073741824 | bytes 10485760 | tf_op jit(solution)/shard_map/update/pallas_call | solution.py:200
  377.4 37.1 %collective-permute-done.28.refs_0_ = bf16[2048,512]{1,0:T(8,128)(2,1)} collective-permute-done((bf16[2048,512]{1,0:T(8,128)(2,1)}, bf16[2048,512]{1,0:T(8,128)(2,1)}, u32[]{:S(2)}, u32[]{:S(2)}) %collective-permute-start.28) | collective-permute-done | bytes 2097184 | tf_op jit(solution)/shard_map/ppermute | solution.py:407
  414.5 6.1 %update.3 = f32[2048,1024]{1,0:T(8,128)} custom-call(f32[2048,512]{1,0:T(8,128)} %get-tuple-element.20.own, bf16[1024,512]{1,0:T(8,128)(2,1)} %constant_dynamic-update-slice_fusion.refs_20_.right, bf16[2048,512]{1,0:T(8,128)(2,1)} %collective-permute-done.28.refs_0_, f32[2048,1024]{1,0:T(8,128)} %update.2.refs_1_, ...), custom_call_target="tpu_custom_call", output_to_operand_aliasing={{}: (3, {})} | custom-call | flops 1073741824 | bytes 10485760 | tf_op jit(solution)/shard_map/update/pallas_call | solution.py:200
  420.6 4.3 %fusion.3 = f32[256,2048]{1,0:T(8,128)} fusion(bf16[256,2048]{1,0:T(8,128)(2,1)} %collective-permute-done.40, bf16[256,2048]{1,0:T(8,128)(2,1)} %collective-permute-done.39, bf16[256,2048]{1,0:T(8,128)(2,1)} %collective-permute-done.38, f32[256,2048]{1,0:T(8,128)S(1)} %copy-done.5, bf16[8,256,2048]{2,1,0:T(8,128)(2,1)} %left_gram.3.refs_25_, s32[]{:T(128)S(6)} %select_n.184), kind=kLoop, calls=%fused_computation.4 | loop fusion | flops 5242880 | bytes 8388612 | tf_op jit(solution)/shard_map/add | solution.py:448
  (111 shorter events, 31.7 us)
Async XLA Ops:
  0.6 47.6 %collective-permute-start.5 = (bf16[256,2048]{1,0:T(8,128)(2,1)}, bf16[256,2048]{1,0:T(8,128)(2,1)S(1)}, u32[]{:S(2)}, u32[]{:S(2)}) collective-permute-start(bf16[256,2048]{1,0:T(8,128)(2,1)} %refs_0_.3), channel_id=1, source_target_pairs={{0,8},{2,10},{4,12},{6,14},{8,16},{10,18},{12,20},{14,22},{16,24},... | collective-permute-start | bytes 3145736 | tf_op jit(solution)/shard_map/ppermute | solution.py:318
  0.7 50.8 %collective-permute-start.3 = (bf16[256,2048]{1,0:T(8,128)(2,1)}, bf16[256,2048]{1,0:T(8,128)(2,1)S(1)}, u32[]{:S(2)}, u32[]{:S(2)}) collective-permute-start(bf16[256,2048]{1,0:T(8,128)(2,1)} %refs_0_.3), channel_id=1, source_target_pairs={{0,24},{2,26},{4,28},{6,30},{8,0},{10,2},{12,4},{14,6},{16,8},{18,... | collective-permute-start | bytes 3145736 | tf_op jit(solution)/shard_map/ppermute | solution.py:318
  2.7 49.3 %collective-permute-start.1 = (bf16[256,2048]{1,0:T(8,128)(2,1)}, bf16[256,2048]{1,0:T(8,128)(2,1)}, u32[]{:S(2)}, u32[]{:S(2)}) collective-permute-start(bf16[256,2048]{1,0:T(8,128)(2,1)} %refs_0_.3), channel_id=1, source_target_pairs={{0,4},{2,6},{4,0},{6,2},{8,12},{10,14},{12,8},{14,10},{16,20},{18,... | collective-permute-start | bytes 3145736 | tf_op jit(solution)/shard_map/ppermute | solution.py:318
  4.2 48.3 %collective-permute-start = (bf16[256,2048]{1,0:T(8,128)(2,1)}, bf16[256,2048]{1,0:T(8,128)(2,1)S(1)}, u32[]{:S(2)}, u32[]{:S(2)}) collective-permute-start(bf16[256,2048]{1,0:T(8,128)(2,1)} %refs_0_.3), channel_id=1, source_target_pairs={{0,2},{2,0},{4,6},{6,4},{8,10},{10,8},{12,14},{14,12},{16,18},{18,... | collective-permute-start | bytes 3145736 | tf_op jit(solution)/shard_map/ppermute | solution.py:318
  4.2 45.7 %collective-permute-start.19 = (bf16[1024,256]{1,0:T(8,128)(2,1)}, bf16[1024,256]{1,0:T(8,128)(2,1)S(1)}, u32[]{:S(2)}, u32[]{:S(2)}) collective-permute-start(bf16[1024,256]{1,0:T(8,128)(2,1)} %param.11), channel_id=1, source_target_pairs={{1,0},{0,1},{3,2},{2,3},{5,4},{4,5},{7,6},{6,7},{9,8},{8,9},{11,10... | collective-permute-start | bytes 1572872 | tf_op jit(solution)/shard_map/ppermute | solution.py:404
  49.9 48.7 %collective-permute-start.21 = (bf16[2048,512]{1,0:T(8,128)(2,1)S(1)}, bf16[2048,512]{1,0:T(8,128)(2,1)}, u32[]{:S(2)}, u32[]{:S(2)}) collective-permute-start(bf16[2048,512]{1,0:T(8,128)(2,1)S(1)} %get-tuple-element.40.refs_0_.refs_4_.refs_21_.refs_1_), channel_id=1, source_target_pairs={{1,0},{0,1},{3,2},{2,3},{5,4},{4,5},{7,6},{6,7},{9,8},{8,9},{11,10... | collective-permute-start | bytes 6291464 | tf_op jit(solution)/shard_map/ppermute | solution.py:404
  51.5 91.5 %collective-permute-start.20 = (bf16[2048,512]{1,0:T(8,128)(2,1)}, bf16[2048,512]{1,0:T(8,128)(2,1)}, u32[]{:S(2)}, u32[]{:S(2)}) collective-permute-start(bf16[2048,512]{1,0:T(8,128)(2,1)} %get-tuple-element.41.refs_1_.refs_5_.refs_21_.refs_0_), channel_id=1, source_target_pairs={{1,0},{0,1},{3,2},{2,3},{5,4},{4,5},{7,6},{6,7},{9,8},{8,9},{11,10... | collective-permute-start | bytes 6291464 | tf_op jit(solution)/shard_map/ppermute | solution.py:404
  52.0 26.8 %collective-permute-start.11 = (bf16[256,2048]{1,0:T(8,128)(2,1)S(1)}, bf16[256,2048]{1,0:T(8,128)(2,1)}, u32[]{:S(2)}, u32[]{:S(2)}) collective-permute-start(bf16[256,2048]{1,0:T(8,128)(2,1)S(1)} %collective-permute-done.3.refs_4_), channel_id=1, source_target_pairs={{0,24},{2,26},{4,28},{6,30},{8,0},{10,2},{12,4},{14,6},{16,8},{18,... | collective-permute-start | bytes 3145736 | tf_op jit(solution)/shard_map/ppermute | solution.py:318
  52.5 26.4 %collective-permute-start.9 = (bf16[256,2048]{1,0:T(8,128)(2,1)S(1)}, bf16[256,2048]{1,0:T(8,128)(2,1)}, u32[]{:S(2)}, u32[]{:S(2)}) collective-permute-start(bf16[256,2048]{1,0:T(8,128)(2,1)S(1)} %collective-permute-done.3.refs_4_), channel_id=1, source_target_pairs={{0,4},{2,6},{4,0},{6,2},{8,12},{10,14},{12,8},{14,10},{16,20},{18,... | collective-permute-start | bytes 3145736 | tf_op jit(solution)/shard_map/ppermute | solution.py:318
  54.0 25.4 %collective-permute-start.4 = (bf16[256,2048]{1,0:T(8,128)(2,1)S(1)}, bf16[256,2048]{1,0:T(8,128)(2,1)S(1)}, u32[]{:S(2)}, u32[]{:S(2)}) collective-permute-start(bf16[256,2048]{1,0:T(8,128)(2,1)S(1)} %collective-permute-done.3.refs_4_), channel_id=1, source_target_pairs={{0,2},{2,0},{4,6},{6,4},{8,10},{10,8},{12,14},{14,12},{16,18},{18,... | collective-permute-start | bytes 3145736 | tf_op jit(solution)/shard_map/ppermute | solution.py:318
  78.9 70.9 %collective-permute-start.24 = (bf16[2048,512]{1,0:T(8,128)(2,1)S(1)}, bf16[2048,512]{1,0:T(8,128)(2,1)}, u32[]{:S(2)}, u32[]{:S(2)}) collective-permute-start(bf16[2048,512]{1,0:T(8,128)(2,1)S(1)} %get-tuple-element.40.refs_0_.refs_4_.refs_21_.refs_1_), channel_id=1, source_target_pairs={{0,2},{2,0},{4,6},{6,4},{8,10},{10,8},{12,14},{14,12},{16,18},{18,... | collective-permute-start | bytes 6291464 | tf_op jit(solution)/shard_map/ppermute | solution.py:318
  78.9 71.4 %collective-permute-start.25 = (bf16[2048,512]{1,0:T(8,128)(2,1)}, bf16[2048,512]{1,0:T(8,128)(2,1)}, u32[]{:S(2)}, u32[]{:S(2)}) collective-permute-start(bf16[2048,512]{1,0:T(8,128)(2,1)} %get-tuple-element.41.refs_1_.refs_5_.refs_21_.refs_0_), channel_id=1, source_target_pairs={{0,2},{2,0},{4,6},{6,4},{8,10},{10,8},{12,14},{14,12},{16,18},{18,... | collective-permute-start | bytes 6291464 | tf_op jit(solution)/shard_map/ppermute | solution.py:318
  79.4 66.0 %collective-permute-start.7 = (bf16[256,2048]{1,0:T(8,128)(2,1)}, bf16[256,2048]{1,0:T(8,128)(2,1)}, u32[]{:S(2)}, u32[]{:S(2)}) collective-permute-start(bf16[256,2048]{1,0:T(8,128)(2,1)} %collective-permute-done.1.refs_2_), channel_id=1, source_target_pairs={{0,8},{2,10},{4,12},{6,14},{8,16},{10,18},{12,20},{14,22},{16,24},... | collective-permute-start | bytes 3145736 | tf_op jit(solution)/shard_map/ppermute | solution.py:318
  98.6 73.5 %collective-permute-start.22 = (bf16[2048,512]{1,0:T(8,128)(2,1)}, bf16[2048,512]{1,0:T(8,128)(2,1)}, u32[]{:S(2)}, u32[]{:S(2)}) collective-permute-start(bf16[2048,512]{1,0:T(8,128)(2,1)} %collective-permute-done.21.refs_0_.refs_22_.refs_2_.refs_3_), channel_id=1, source_target_pairs={{0,2},{2,0},{4,6},{6,4},{8,10},{10,8},{12,14},{14,12},{16,18},{18,... | collective-permute-start | bytes 6291464 | tf_op jit(solution)/shard_map/ppermute | solution.py:318
  143.0 29.2 %collective-permute-start.23 = (bf16[2048,512]{1,0:T(8,128)(2,1)}, bf16[2048,512]{1,0:T(8,128)(2,1)}, u32[]{:S(2)}, u32[]{:S(2)}) collective-permute-start(bf16[2048,512]{1,0:T(8,128)(2,1)} %collective-permute-done.20.refs_1_.refs_22_.refs_2_.refs_3_), channel_id=1, source_target_pairs={{0,2},{2,0},{4,6},{6,4},{8,10},{10,8},{12,14},{14,12},{16,18},{18,... | collective-permute-start | bytes 6291464 | tf_op jit(solution)/shard_map/ppermute | solution.py:318
  145.4 24.6 %collective-permute-start.2 = (bf16[256,2048]{1,0:T(8,128)(2,1)}, bf16[256,2048]{1,0:T(8,128)(2,1)}, u32[]{:S(2)}, u32[]{:S(2)}) collective-permute-start(bf16[256,2048]{1,0:T(8,128)(2,1)} %collective-permute-done.1.refs_2_), channel_id=1, source_target_pairs={{0,2},{2,0},{4,6},{6,4},{8,10},{10,8},{12,14},{14,12},{16,18},{18,... | collective-permute-start | bytes 3145736 | tf_op jit(solution)/shard_map/ppermute | solution.py:318
  171.6 29.3 %collective-permute-start.12 = (bf16[256,2048]{1,0:T(8,128)(2,1)}, bf16[256,2048]{1,0:T(8,128)(2,1)}, u32[]{:S(2)}, u32[]{:S(2)}) collective-permute-start(bf16[256,2048]{1,0:T(8,128)(2,1)} %collective-permute-done.11.refs_12_), channel_id=1, source_target_pairs={{0,2},{2,0},{4,6},{6,4},{8,10},{10,8},{12,14},{14,12},{16,18},{18,... | collective-permute-start | bytes 3145736 | tf_op jit(solution)/shard_map/ppermute | solution.py:318
  171.6 30.9 %collective-permute-start.10 = (bf16[256,2048]{1,0:T(8,128)(2,1)}, bf16[256,2048]{1,0:T(8,128)(2,1)}, u32[]{:S(2)}, u32[]{:S(2)}) collective-permute-start(bf16[256,2048]{1,0:T(8,128)(2,1)} %collective-permute-done.9.refs_10_), channel_id=1, source_target_pairs={{0,2},{2,0},{4,6},{6,4},{8,10},{10,8},{12,14},{14,12},{16,18},{18,... | collective-permute-start | bytes 3145736 | tf_op jit(solution)/shard_map/ppermute | solution.py:318
  172.1 32.8 %collective-permute-start.8 = (bf16[256,2048]{1,0:T(8,128)(2,1)}, bf16[256,2048]{1,0:T(8,128)(2,1)}, u32[]{:S(2)}, u32[]{:S(2)}) collective-permute-start(bf16[256,2048]{1,0:T(8,128)(2,1)} %collective-permute-done.7.refs_8_), channel_id=1, source_target_pairs={{0,2},{2,0},{4,6},{6,4},{8,10},{10,8},{12,14},{14,12},{16,18},{18,... | collective-permute-start | bytes 3145736 | tf_op jit(solution)/shard_map/ppermute | solution.py:318
  195.0 129.0 %collective-permute-start.36 = (bf16[256,2048]{1,0:T(8,128)(2,1)S(1)}, bf16[256,2048]{1,0:T(8,128)(2,1)}, u32[]{:S(2)}, u32[]{:S(2)}) collective-permute-start(bf16[256,2048]{1,0:T(8,128)(2,1)S(1)} %get-tuple-element.28), channel_id=1, source_target_pairs={{8,12},{10,14},{12,8},{14,10},{16,20},{18,22},{20,16},{22,18},{24,... | collective-permute-start | bytes 3145736 | tf_op jit(solution)/shard_map/ppermute | solution.py:326
  197.5 115.1 %collective-permute-start.32 = (bf16[256,2048]{1,0:T(8,128)(2,1)S(1)}, bf16[256,2048]{1,0:T(8,128)(2,1)}, u32[]{:S(2)}, u32[]{:S(2)}) collective-permute-start(bf16[256,2048]{1,0:T(8,128)(2,1)S(1)} %get-tuple-element.30), channel_id=1, source_target_pairs={{16,20},{18,22},{20,16},{22,18},{24,28},{26,30},{28,24},{30,26},{1... | collective-permute-start | bytes 3145736 | tf_op jit(solution)/shard_map/ppermute | solution.py:326
  200.9 113.3 %collective-permute-start.30 = (bf16[256,2048]{1,0:T(8,128)(2,1)S(1)}, bf16[256,2048]{1,0:T(8,128)(2,1)}, u32[]{:S(2)}, u32[]{:S(2)}) collective-permute-start(bf16[256,2048]{1,0:T(8,128)(2,1)S(1)} %get-tuple-element.31), channel_id=1, source_target_pairs={{0,4},{2,6},{4,0},{6,2},{8,12},{10,14},{12,8},{14,10},{1,5},{3,7},... | collective-permute-start | bytes 3145736 | tf_op jit(solution)/shard_map/ppermute | solution.py:326
  202.5 64.6 %collective-permute-start.27 = (bf16[256,2048]{1,0:T(8,128)(2,1)}, bf16[256,2048]{1,0:T(8,128)(2,1)}, u32[]{:S(2)}, u32[]{:S(2)}) collective-permute-start(bf16[256,2048]{1,0:T(8,128)(2,1)} %get-tuple-element.32), channel_id=1, source_target_pairs={{24,28},{26,30},{28,24},{30,26},{25,29},{27,31},{29,25},{31,27}} | collective-permute-start | bytes 3145736 | tf_op jit(solution)/shard_map/ppermute | solution.py:326
  205.0 62.1 %collective-permute-start.26 = (bf16[256,2048]{1,0:T(8,128)(2,1)S(1)}, bf16[256,2048]{1,0:T(8,128)(2,1)}, u32[]{:S(2)}, u32[]{:S(2)}) collective-permute-start(bf16[256,2048]{1,0:T(8,128)(2,1)S(1)} %get-tuple-element.33), channel_id=1, source_target_pairs={{0,4},{2,6},{4,0},{6,2},{1,5},{3,7},{5,1},{7,3}} | collective-permute-start | bytes 3145736 | tf_op jit(solution)/shard_map/ppermute | solution.py:326
  271.2 43.0 %collective-permute-start.33 = (bf16[256,2048]{1,0:T(8,128)(2,1)}, bf16[256,2048]{1,0:T(8,128)(2,1)}, u32[]{:S(2)}, u32[]{:S(2)}) collective-permute-start(bf16[256,2048]{1,0:T(8,128)(2,1)} %get-tuple-element.38.refs_28_), channel_id=1, source_target_pairs={{24,16},{26,18},{28,20},{30,22},{25,17},{27,19},{29,21},{31,23}} | collective-permute-start | bytes 3145736 | tf_op jit(solution)/shard_map/ppermute | solution.py:326
  273.5 40.7 %collective-permute-start.31 = (bf16[256,2048]{1,0:T(8,128)(2,1)S(1)}, bf16[256,2048]{1,0:T(8,128)(2,1)}, u32[]{:S(2)}, u32[]{:S(2)}) collective-permute-start(bf16[256,2048]{1,0:T(8,128)(2,1)S(1)} %get-tuple-element.39.refs_27_), channel_id=1, source_target_pairs={{0,8},{2,10},{4,12},{6,14},{1,9},{3,11},{5,13},{7,15}} | collective-permute-start | bytes 3145736 | tf_op jit(solution)/shard_map/ppermute | solution.py:326
  318.3 23.4 %collective-permute-start.37 = (bf16[256,2048]{1,0:T(8,128)(2,1)S(1)}, bf16[256,2048]{1,0:T(8,128)(2,1)}, u32[]{:S(2)}, u32[]{:S(2)}) collective-permute-start(bf16[256,2048]{1,0:T(8,128)(2,1)S(1)} %get-tuple-element.36.refs_2_.refs_5_.refs_6_), channel_id=1, source_target_pairs={{16,8},{18,10},{20,12},{22,14},{24,16},{26,18},{28,20},{30,22},{17... | collective-permute-start | bytes 3145736 | tf_op jit(solution)/shard_map/ppermute | solution.py:326
  322.4 48.9 %collective-permute-start.29 = (bf16[2048,512]{1,0:T(8,128)(2,1)}, bf16[2048,512]{1,0:T(8,128)(2,1)}, u32[]{:S(2)}, u32[]{:S(2)}) collective-permute-start(bf16[2048,512]{1,0:T(8,128)(2,1)} %get-tuple-element.22), channel_id=1, source_target_pairs={{0,1},{1,0},{2,3},{3,2},{4,5},{5,4},{6,7},{7,6},{8,9},{9,8},{10,11... | collective-permute-start | bytes 6291464 | tf_op jit(solution)/shard_map/ppermute | solution.py:407
  324.0 90.5 %collective-permute-start.28 = (bf16[2048,512]{1,0:T(8,128)(2,1)}, bf16[2048,512]{1,0:T(8,128)(2,1)}, u32[]{:S(2)}, u32[]{:S(2)}) collective-permute-start(bf16[2048,512]{1,0:T(8,128)(2,1)} %get-tuple-element.21), channel_id=1, source_target_pairs={{0,1},{1,0},{2,3},{3,2},{4,5},{5,4},{6,7},{7,6},{8,9},{9,8},{10,11... | collective-permute-start | bytes 6291464 | tf_op jit(solution)/shard_map/ppermute | solution.py:407
  335.5 85.1 %collective-permute-start.38 = (bf16[256,2048]{1,0:T(8,128)(2,1)S(1)}, bf16[256,2048]{1,0:T(8,128)(2,1)}, u32[]{:S(2)}, u32[]{:S(2)}) collective-permute-start(bf16[256,2048]{1,0:T(8,128)(2,1)S(1)} %get-tuple-element.27), channel_id=1, source_target_pairs={{0,4},{2,6},{4,0},{6,2},{8,12},{10,14},{12,8},{14,10},{16,20},{18,... | collective-permute-start | bytes 3145736 | tf_op jit(solution)/shard_map/ppermute | solution.py:326
  345.8 74.9 %collective-permute-start.40 = (bf16[256,2048]{1,0:T(8,128)(2,1)S(1)}, bf16[256,2048]{1,0:T(8,128)(2,1)}, u32[]{:S(2)}, u32[]{:S(2)}) collective-permute-start(bf16[256,2048]{1,0:T(8,128)(2,1)S(1)} %get-tuple-element.34.refs_3_), channel_id=1, source_target_pairs={{8,0},{10,2},{12,4},{14,6},{16,8},{18,10},{20,12},{22,14},{24,16},... | collective-permute-start | bytes 3145736 | tf_op jit(solution)/shard_map/ppermute | solution.py:326
  351.2 69.4 %collective-permute-start.39 = (bf16[256,2048]{1,0:T(8,128)(2,1)S(1)}, bf16[256,2048]{1,0:T(8,128)(2,1)}, u32[]{:S(2)}, u32[]{:S(2)}) collective-permute-start(bf16[256,2048]{1,0:T(8,128)(2,1)S(1)} %get-tuple-element.35.refs_2_), channel_id=1, source_target_pairs={{0,8},{2,10},{4,12},{6,14},{8,16},{10,18},{12,20},{14,22},{16,24},... | collective-permute-start | bytes 3145736 | tf_op jit(solution)/shard_map/ppermute | solution.py:326
  (27 other events, 790.3 us)

commit v2 on v1

--- a/solution.py
+++ b/solution.py
@@ -53,18 +53,16 @@
     step = pl.program_id(0)
     lead = sections * fill
 
-    def load(c):
-        lanes = pl.ds(c * tile, tile)
+    @pl.when((step == 0) | ((step >= lead - 1) & (step < lead + turn - 2)))
+    def _():
+        c = jnp.where(step == 0, 0, step - lead + 2)
+        lanes = pl.ds(pl.multiple_of(c * tile, tile), tile)
         for k in range(pieces):
             rows = lefts[k].shape[0]
             base = pl.multiple_of(at_ref[k], 16)
-            pltpu.make_async_copy(lefts[k].at[:, lanes], left.at[pl.ds(base, rows), lanes], sems.at[c]).start()
-
-    for c in range(turn):
-
-        @pl.when(step == min(c, lead - 1))
-        def _(c=c):
-            load(c)
+            pltpu.make_async_copy(
+                lefts[k].at[:, lanes], left.at[pl.ds(base, rows), lanes], sems.at[c]
+            ).start()
 
     for k in range(sections):
 
@@ -73,20 +71,19 @@
             base = pl.multiple_of((s_ref[k] * fill + step - k * fill) * part, part)
             turned[pl.ds(base, part), :] = dot(grads[k][...], right[...], 1, 0).astype(BF16)
 
-    for c in range(turn):
-
-        @pl.when(step == lead + c)
-        def _(c=c):
-            lanes = pl.ds(c * tile, tile)
-            pltpu.make_async_copy(left.at[:, lanes], left.at[:, lanes], sems.at[c]).wait()
-            rotated = dot(left[:, lanes], turned[...], 0, 0)
-            first = decay * avg[...] + (1.0 - decay) * rotated
-            second = decay * avg_sq[...] + (1.0 - decay) * rotated * rotated
-            first_out[...] = first
-            second_out[...] = second
-            direction[lanes, :] = (
-                first / bias_fix / (jnp.sqrt(second / bias_fix) + 1e-08)
-            ).astype(BF16)
+    @pl.when((step >= lead) & (step < lead + turn))
+    def _():
+        c = step - lead
+        lanes = pl.ds(pl.multiple_of(c * tile, tile), tile)
+        pltpu.make_async_copy(left.at[:, lanes], left.at[:, lanes], sems.at[c]).wait()
+        rotated = dot(left[:, lanes], turned[...], 0, 0)
+        first = decay * avg[...] + (1.0 - decay) * rotated
+        second = decay * avg_sq[...] + (1.0 - decay) * rotated * rotated
+        first_out[...] = first
+        second_out[...] = second
+        direction[lanes, :] = (
+            first * (1.0 / bias_fix) / (jnp.sqrt(second * (1.0 / bias_fix)) + 1e-08)
+        ).astype(BF16)
 
     spin = step - lead - turn
     split = (sections - 1) * strips
@@ -117,6 +114,7 @@
     fill, turn, strips = rows // part, rows // tile, rows // strip
     lead = sections * fill
     split = max(sections - 1, 1) * strips
+    assert lead > 1
 
     def column(i, s, a):
         return (jnp.clip(i - lead, 0, turn - 1), b)
@@ -366,27 +364,48 @@
 
 
 class Reduction:
-    def __init__(self, at, parts):
-        self.at, self.parts = at, parts
-        self.offsets = [dz for t in range(at.outer - 1, 0, -1) for dz in (t, -t)] + [0]
-        self.came = {}
-        for dz in self.offsets:
-            self.came[dz] = [at.pass_on(self.part(dz, 1), dy=1, only=dz)]
-
-    def part(self, dz, dy):
-        return lax.dynamic_index_in_dim(self.parts, self.at.chip(dz, dy), 0, keepdims=False)
-
-    def total(self, dz):
-        total = self.part(dz, 0).astype(F32)
+    def __init__(self, at, sections):
+        self.at, self.sections = at, sections
+        self.came = {dz: [] for dz in range(1 - at.outer, at.outer)}
+        self.across = []
+
+    def add(self, s, parts):
+        at, section, mine = self.at, self.sections[s], self.sections[0]
+        self.parts = parts
+        count = at.outer // len(self.sections)
+        sent = []
+        for k in range(count):
+            step = jnp.where(section > mine, count - 1 - k, k)
+            place = section * count + step
+            slab = lax.dynamic_index_in_dim(parts, place * 2 + 1 - at.y, 0, keepdims=False)
+            self.across.append((s, k, place, at.send(slab, dy=1)))
+            sent.append(slab)
+        return tuple(sent)
+
+    def held(self, dz):
+        outer = self.at.outer
+        place = jnp.clip(self.at.z + dz, 0, outer - 1)
+        total = lax.dynamic_index_in_dim(self.parts, place * 2 + self.at.y, 0, keepdims=False).astype(F32)
+        across = None
+        for s, k, where, x in self.across:
+            if s > 0 and k > 0 and abs(dz) == outer - 1:
+                continue
+            across = x if across is None else jnp.where(place == where, x, across)
+        return total + across.astype(F32)
+
+    def arrived(self, total, dz, scale=1.0):
         for x in self.came[dz]:
-            total = total + x.astype(F32)
+            total = total + scale * x.astype(F32)
         return total
 
     def round(self, t, after):
         self.parts, _ = lax.optimization_barrier((self.parts, after))
         sent = []
         for dz, way in ((t, 1), (-t, -1)):
-            sent.append(self.total(dz).astype(BF16))
+            total = self.held(dz)
+            if t == 1:
+                total = lax.optimization_barrier(total)
+            sent.append(self.arrived(total, dz).astype(BF16))
             self.came[dz - way].append(self.at.pass_on(sent[-1], dz=way, only=dz))
         return tuple(sent)
 
@@ -425,12 +444,12 @@
     sides = [grads[b][0] for b in blocks] + [twins[b][0] for b in blocks]
     parts = moments = update = right_stat = None
     kept, came, after = [], [], ()
+    sums = Reduction(at, sections)
     for s in range(col_count):
         tops = [grads[k][s] for k in blocks] + [twins[k][s] for k in blocks]
-        parts = left_gram(sections[s], at.core, slab, at.count // 2, tops, sides, parts)
-    sums = Reduction(at, parts)
+        parts = left_gram(sections[s], at.core, slab, at.count // 2, tops, sides, parts, after)
+        after = sums.add(s, parts)
     rounds = list(range(at.outer - 1, 0, -1))
-    after = (parts,)
     for b in blocks:
         first, second, shared, share = block(
             b, order, left, right, grads[b], exp_avg, exp_avg_sq, moments, after
@@ -445,7 +464,8 @@
         update = update_block(b, kept[b], came[b], right, cols_here, update, after)
     while rounds:
         after = sums.round(rounds.pop(0), right_stat)
-    left_stat = decay * gram_left + (1.0 - decay) * sums.total(0)
+    base = lax.optimization_barrier(decay * gram_left + (1.0 - decay) * sums.held(0))
+    left_stat = sums.arrived(base, 0, 1.0 - decay)
     update = update_block(blocks[-1], kept[-1], came[-1], right, cols_here, update, after)
     return (update, *moments, left_stat, right_stat)
 

time: 432 us -> 398 us (0.921)
  the two profiles are of different devices: /device:TPU:24 before, /device:TPU:0 now
where the time goes in v2:
time: 398 us; the launch traced here: 397 us
  waiting for transfers between devices  188 us (47%)
  Pallas kernels  124 us (31%)
  starting transfers between devices  43.3 us (11%)
  other arithmetic  26.9 us (7%)
  local copies, waits for them, and re-layouts  14.1 us (4%)
    pallas_call x2, Pallas kernels, block(): pl.pallas_call(functools.partial(block_kernel, pieces, sections, fill, tu...  70.2 us
    ppermute x3, waiting for transfers between devices, from_right(): lax.ppermute(x, 'col', [((i + s) % col_count, i) for i in range(col_count)])  69.4 us
    ppermute x27, waiting for transfers between devices, send(): return lax.ppermute(x, 'grp', pairs)  65 us
    ppermute x2, waiting for transfers between devices, to_right(): lax.ppermute(x, 'col', [(i, (i + s) % col_count) for i in range(col_count)])  53.7 us
    pallas_call x2, Pallas kernels, left_gram(): pl.pallas_call(functools.partial(gram_kernel, pieces), grid_spec=pltpu.Pr...  30.4 us
    ppermute x27, starting transfers between devices, send(): return lax.ppermute(x, 'grp', pairs)  23.4 us
    ppermute x6, starting transfers between devices, pass_on(): return lax.ppermute(x, 'grp', pairs)  13.7 us
    pallas_call x2, Pallas kernels, update_block(): pl.pallas_call(functools.partial(update_kernel, len(parts)), grid=(rows /...  12.2 us
  transfers between devices with their start and end apart: 38, of which 11 were waited for; matrix products, arithmetic and copies ran while one was open for 8% of the time, Pallas kernels for 31%

profile of v2, /device:TPU:0, one launch (start us, length us, event | category | flops | bytes accessed | tf_op | source)
XLA Modules:
  0.0 397.2 jit_solution(9009704910180047771)
XLA Ops:
  0.6 5.1 %collective-permute-start.3 = (bf16[256,2048]{1,0:T(8,128)(2,1)}, bf16[256,2048]{1,0:T(8,128)(2,1)}, u32[]{:S(2)}, u32[]{:S(2)}) collective-permute-start(bf16[256,2048]{1,0:T(8,128)(2,1)} %refs_0_.3), channel_id=1, source_target_pairs={{0,24},{2,26},{4,28},{6,30},{8,0},{10,2},{12,4},{14,6},{16,8},{18,... | collective-permute-start | bytes 3145736 | tf_op jit(solution)/shard_map/ppermute | solution.py:316
  8.8 4.0 %convert.11 = bf16[2048,1024]{1,0:T(8,128)(2,1)S(1)} convert(f32[2048,1024]{1,0:T(8,128)} %param.7) | non-fusion elementwise | flops 2097152 | bytes 12582912 | tf_op jit(solution)/shard_map/convert.8
  13.2 7.4 %collective-permute-done.19 = bf16[1024,256]{1,0:T(8,128)(2,1)S(1)} collective-permute-done((bf16[1024,256]{1,0:T(8,128)(2,1)}, bf16[1024,256]{1,0:T(8,128)(2,1)S(1)}, u32[]{:S(2)}, u32[]{:S(2)}) %collective-permute-start.19) | collective-permute-done | bytes 524320 | tf_op jit(solution)/shard_map/ppermute | solution.py:423
  20.6 9.0 %collective-permute-done.3.refs_4_ = bf16[256,2048]{1,0:T(8,128)(2,1)} collective-permute-done((bf16[256,2048]{1,0:T(8,128)(2,1)}, bf16[256,2048]{1,0:T(8,128)(2,1)}, u32[]{:S(2)}, u32[]{:S(2)}) %collective-permute-start.3) | collective-permute-done | bytes 1048608 | tf_op jit(solution)/shard_map/ppermute | solution.py:316
  32.2 19.7 %collective-permute-done.5.refs_6_ = bf16[256,2048]{1,0:T(8,128)(2,1)} collective-permute-done((bf16[256,2048]{1,0:T(8,128)(2,1)}, bf16[256,2048]{1,0:T(8,128)(2,1)}, u32[]{:S(2)}, u32[]{:S(2)}) %collective-permute-start.5) | collective-permute-done | bytes 1048608 | tf_op jit(solution)/shard_map/ppermute | solution.py:316
  51.9 2.7 collective-permute-done.refs_1_
  54.5 3.0 collective-permute-start.11
  58.1 20.1 %collective-permute-done.21.refs_0_.refs_22_.refs_2_.refs_3_ = bf16[2048,512]{1,0:T(8,128)(2,1)} collective-permute-done((bf16[2048,512]{1,0:T(8,128)(2,1)S(1)}, bf16[2048,512]{1,0:T(8,128)(2,1)}, u32[]{:S(2)}, u32[]{:S(2)}) %collective-permute-start.21) | collective-permute-done | bytes 2097184 | tf_op jit(solution)/shard_map/ppermute | solution.py:423
  78.2 41.9 %collective-permute-done.20.refs_1_.refs_22_.refs_2_.refs_3_ = bf16[2048,512]{1,0:T(8,128)(2,1)} collective-permute-done((bf16[2048,512]{1,0:T(8,128)(2,1)S(1)}, bf16[2048,512]{1,0:T(8,128)(2,1)}, u32[]{:S(2)}, u32[]{:S(2)}) %collective-permute-start.20) | collective-permute-done | bytes 2097184 | tf_op jit(solution)/shard_map/ppermute | solution.py:423
  124.2 4.3 %collective-permute-start.17 = (bf16[80,2048]{1,0:T(8,128)(2,1)S(1)}, bf16[80,2048]{1,0:T(8,128)(2,1)S(1)}, u32[]{:S(2)}, u32[]{:S(2)}) collective-permute-start(bf16[80,2048]{1,0:T(8,128)(2,1)S(1)} %slice.24), channel_id=1, source_target_pairs={{0,24},{2,26},{4,28},{6,30},{8,0},{10,2},{12,4},{14,6},{16,8},{18,... | collective-permute-start | bytes 983048 | tf_op jit(solution)/shard_map/ppermute | solution.py:316
  134.5 2.1 collective-permute-done.17.refs_18_
  136.6 15.2 %left_gram.2.refs_8_ = bf16[8,256,2048]{2,1,0:T(8,128)(2,1)} custom-call(s32[2]{0:T(128)} %pad_add_fusion.2.s_ref, bf16[2048,512]{1,0:T(8,128)(2,1)} %copy-done, bf16[2048,512]{1,0:T(8,128)(2,1)} %copy-done.1, bf16[2048,512]{1,0:T(8,128)(2,1)} %copy-done.13, bf16[2048,512]{1,0:T(8,128)(2,1)} %copy-done.14, bf16[2048,512]{1,0:T(8,128)(2,1)} %copy-done, ...), custom_call_target="tpu_custom_call" | custom-call | flops 8589934592 | bytes 20971520 | tf_op jit(solution)/shard_map/left_gram/pallas_call | solution.py:235
  151.8 3.1 dynamic-slice_bitcast_fusion.2
  156.5 15.2 %left_gram.3 = bf16[8,256,2048]{2,1,0:T(8,128)(2,1)} custom-call(s32[2]{0:T(128)} %pad_add_fusion.1.s_ref, bf16[2048,512]{1,0:T(8,128)(2,1)} %collective-permute-done.21.refs_0_.refs_22_.refs_2_.refs_3_, bf16[2048,512]{1,0:T(8,128)(2,1)} %collective-permute-done.20.refs_1_.refs_22_.refs_2_.refs_3_, ...), custom_call_target="tpu_custom_call", output_to_operand_aliasing={{}: (9, {})} | custom-call | flops 8589934592 | bytes 20971520 | tf_op jit(solution)/shard_map/left_gram/pallas_call | solution.py:235
  171.7 3.2 dynamic-slice_bitcast_fusion
  179.6 35.1 %block.2 = (f32[2048,1024]{1,0:T(8,128)}, f32[2048,1024]{1,0:T(8,128)}, bf16[2048,512]{1,0:T(8,128)(2,1)}, f32[2048,512]{1,0:T(8,128)}) custom-call(s32[2]{0:T(128)} %pad_add_fusion.s_ref, s32[20]{0:T(128)} %stack.111.at_ref, bf16[256,2048]{1,0:T(8,128)(2,1)} %refs_0_.3, bf16[256,2048]{1,0:T(8,128)(2,1)} %copy-done.18, ...), custom_call_target="tpu_custom_call" | custom-call | flops 21474836480 | bytes 46137344 | tf_op jit(solution)/shard_map/block/pallas_call | solution.py:140
  214.7 8.9 %collective-permute-done.28 = bf16[256,2048]{1,0:T(8,128)(2,1)S(1)} collective-permute-done((bf16[256,2048]{1,0:T(8,128)(2,1)S(1)}, bf16[256,2048]{1,0:T(8,128)(2,1)S(1)}, u32[]{:S(2)}, u32[]{:S(2)}) %collective-permute-start.28) | collective-permute-done | bytes 1048608 | tf_op jit(solution)/shard_map/ppermute | solution.py:316
  223.6 22.5 %collective-permute-done.26 = bf16[256,2048]{1,0:T(8,128)(2,1)S(1)} collective-permute-done((bf16[256,2048]{1,0:T(8,128)(2,1)}, bf16[256,2048]{1,0:T(8,128)(2,1)S(1)}, u32[]{:S(2)}, u32[]{:S(2)}) %collective-permute-start.26) | collective-permute-done | bytes 1048608 | tf_op jit(solution)/shard_map/ppermute | solution.py:316
  246.1 4.5 %fusion.6 = (bf16[256,2048]{1,0:T(8,128)(2,1)}, bf16[256,2048]{1,0:T(8,128)(2,1)}) fusion(bf16[256,2048]{1,0:T(8,128)(2,1)S(1)} %collective-permute-done.26, bf16[256,2048]{1,0:T(8,128)(2,1)S(1)} %collective-permute-done.27, bf16[256,2048]{1,0:T(8,128)(2,1)S(1)} %collective-permute-done.28, bf16[8,256,2048]{2,1,0:T(8,128)(2,1)} %left_gram.3, ...), kind=kLoop, calls=%fused_computation.12 | loop fusion | flops 6291456 | bytes 7340044 | tf_op jit(solution)/shard_map/convert_element_type | solution.py:408
  253.6 35.1 %block.3 = (f32[2048,1024]{1,0:T(8,128)}, f32[2048,1024]{1,0:T(8,128)}, bf16[2048,512]{1,0:T(8,128)(2,1)}, f32[2048,512]{1,0:T(8,128)}) custom-call(s32[2]{0:T(128)} %pad_add_fusion.s_ref, s32[20]{0:T(128)} %stack.111.at_ref, bf16[256,2048]{1,0:T(8,128)(2,1)} %refs_0_.3, ...), custom_call_target="tpu_custom_call", output_to_operand_aliasing={{0}: (27, {}), {1}: (28, {})} | custom-call | flops 21474836480 | bytes 46137344 | tf_op jit(solution)/shard_map/block/pallas_call | solution.py:140
  290.7 4.5 %fusion.3 = (bf16[256,2048]{1,0:T(8,128)(2,1)S(1)}, bf16[256,2048]{1,0:T(8,128)(2,1)S(1)}) fusion(bf16[256,2048]{1,0:T(8,128)(2,1)} %collective-permute-done.33, bf16[256,2048]{1,0:T(8,128)(2,1)} %copy-done.9, bf16[256,2048]{1,0:T(8,128)(2,1)S(1)} %collective-permute-done.26, bf16[256,2048]{1,0:T(8,128)(2,1)S(1)} %collective-permute-done.27, ...), kind=kLoop, calls=%fused_computation.7 | loop fusion | flops 9437184 | bytes 10485774 | tf_op jit(solution)/shard_map/convert_element_type | solution.py:408
  295.2 1.6 collective-permute-start.35
  298.9 2.3 collective-permute-start.34
  301.2 5.5 %right_stat.2.refs_4_ = f32[1024,256]{1,0:T(8,128)} custom-call(s32[1]{0:T(128)} %bitcast.31.s_ref, f32[1024,256]{1,0:T(8,128)} %gram.3, bf16[2048,512]{1,0:T(8,128)(2,1)} %copy-done, bf16[2048,512]{1,0:T(8,128)(2,1)} %copy-done, bf16[2048,512]{1,0:T(8,128)(2,1)} %collective-permute-done.21.refs_0_.refs_22_.refs_2_.refs_3_, ...), custom_call_target="tpu_custom_call" | custom-call | flops 1073741824 | bytes 8388608 | tf_op jit(solution)/shard_map/right_stat/pallas_call | solution.py:287
  306.7 5.6 %right_stat.3 = f32[1024,256]{1,0:T(8,128)} custom-call(s32[1]{0:T(128)} %bitcast.31.s_ref, f32[1024,256]{1,0:T(8,128)} %gram.3, bf16[2048,512]{1,0:T(8,128)(2,1)} %copy-done.1, bf16[2048,512]{1,0:T(8,128)(2,1)} %copy-done.1, bf16[2048,512]{1,0:T(8,128)(2,1)} %collective-permute-done.20.refs_1_.refs_22_.refs_2_.refs_3_, ...), custom_call_target="tpu_custom_call", output_to_operand_aliasing={{}: (6, {})} | custom-call | flops 1073741824 | bytes 8388608 | tf_op jit(solution)/shard_map/right_stat/pallas_call | solution.py:287
  312.4 5.9 %fusion.1 = (f32[256,2048]{1,0:T(8,128)}, f32[256,2048]{1,0:T(8,128)S(1)}, f32[256,2048]{1,0:T(8,128)S(1)}) fusion(f32[256,2048]{1,0:T(8,128)} %param.12, bf16[256,2048]{1,0:T(8,128)(2,1)} %copy-done.9, bf16[256,2048]{1,0:T(8,128)(2,1)S(1)} %copy-done.7, bf16[256,2048]{1,0:T(8,128)(2,1)S(1)} %collective-permute-done.27, bf16[256,2048]{1,0:T(8,128)(2,1)S(1)} %copy-done.5, ...), kind=kLoop, calls=%fused_computation.2 | loop fusion | flops 11010048 | bytes 15728661 | tf_op jit(solution)/shard_map/add | solution.py:467
  322.7 5.6 %collective-permute-start.36 = (bf16[256,2048]{1,0:T(8,128)(2,1)S(1)}, bf16[256,2048]{1,0:T(8,128)(2,1)}, u32[]{:S(2)}, u32[]{:S(2)}) collective-permute-start(bf16[256,2048]{1,0:T(8,128)(2,1)S(1)} %add_convert_fusion.1.refs_2_), channel_id=1, source_target_pairs={{0,8},{2,10},{4,12},{6,14},{8,16},{10,18},{12,20},{14,22},{16,24},... | collective-permute-start | bytes 3145736 | tf_op jit(solution)/shard_map/ppermute | solution.py:324
  328.2 17.5 %collective-permute-done.30.refs_0_ = bf16[2048,512]{1,0:T(8,128)(2,1)} collective-permute-done((bf16[2048,512]{1,0:T(8,128)(2,1)}, bf16[2048,512]{1,0:T(8,128)(2,1)}, u32[]{:S(2)}, u32[]{:S(2)}) %collective-permute-start.30) | collective-permute-done | bytes 2097184 | tf_op jit(solution)/shard_map/ppermute | solution.py:426
  345.7 6.1 %update.2.refs_1_ = f32[2048,1024]{1,0:T(8,128)} custom-call(f32[2048,512]{1,0:T(8,128)} %get-tuple-element.18.own, bf16[1024,512]{1,0:T(8,128)(2,1)} %constant_dynamic-update-slice_fusion.refs_20_.right, bf16[2048,512]{1,0:T(8,128)(2,1)} %collective-permute-done.30.refs_0_, bf16[256,2048]{1,0:T(8,128)(2,1)} %copy-done.3, bf16[256,2048]{1,0:T(8,128)(2,1)} %copy-done.2), custom_call_target="tpu_custom_call" | custom-call | flops 1073741824 | bytes 10485760 | tf_op jit(solution)/shard_map/update/pallas_call | solution.py:198
  351.8 36.2 %collective-permute-done.29.refs_0_ = bf16[2048,512]{1,0:T(8,128)(2,1)} collective-permute-done((bf16[2048,512]{1,0:T(8,128)(2,1)}, bf16[2048,512]{1,0:T(8,128)(2,1)}, u32[]{:S(2)}, u32[]{:S(2)}) %collective-permute-start.29) | collective-permute-done | bytes 2097184 | tf_op jit(solution)/shard_map/ppermute | solution.py:426
  388.0 6.1 %update.3 = f32[2048,1024]{1,0:T(8,128)} custom-call(f32[2048,512]{1,0:T(8,128)} %get-tuple-element.20.own, bf16[1024,512]{1,0:T(8,128)(2,1)} %constant_dynamic-update-slice_fusion.refs_20_.right, bf16[2048,512]{1,0:T(8,128)(2,1)} %collective-permute-done.29.refs_0_, f32[2048,1024]{1,0:T(8,128)} %update.2.refs_1_, ...), custom_call_target="tpu_custom_call", output_to_operand_aliasing={{}: (3, {})} | custom-call | flops 1073741824 | bytes 10485760 | tf_op jit(solution)/shard_map/update/pallas_call | solution.py:198
  394.1 3.1 multiply_add_fusion
  (122 shorter events, 34.0 us)
Async XLA Ops:
  0.6 29.0 %collective-permute-start.3 = (bf16[256,2048]{1,0:T(8,128)(2,1)}, bf16[256,2048]{1,0:T(8,128)(2,1)}, u32[]{:S(2)}, u32[]{:S(2)}) collective-permute-start(bf16[256,2048]{1,0:T(8,128)(2,1)} %refs_0_.3), channel_id=1, source_target_pairs={{0,24},{2,26},{4,28},{6,30},{8,0},{10,2},{12,4},{14,6},{16,8},{18,... | collective-permute-start | bytes 3145736 | tf_op jit(solution)/shard_map/ppermute | solution.py:316
  5.8 25.4 %collective-permute-start.1 = (bf16[256,2048]{1,0:T(8,128)(2,1)}, bf16[256,2048]{1,0:T(8,128)(2,1)}, u32[]{:S(2)}, u32[]{:S(2)}) collective-permute-start(bf16[256,2048]{1,0:T(8,128)(2,1)} %refs_0_.3), channel_id=1, source_target_pairs={{0,4},{2,6},{4,0},{6,2},{8,12},{10,14},{12,8},{14,10},{16,20},{18,... | collective-permute-start | bytes 3145736 | tf_op jit(solution)/shard_map/ppermute | solution.py:316
  7.3 44.6 %collective-permute-start.5 = (bf16[256,2048]{1,0:T(8,128)(2,1)}, bf16[256,2048]{1,0:T(8,128)(2,1)}, u32[]{:S(2)}, u32[]{:S(2)}) collective-permute-start(bf16[256,2048]{1,0:T(8,128)(2,1)} %refs_0_.3), channel_id=1, source_target_pairs={{0,8},{2,10},{4,12},{6,14},{8,16},{10,18},{12,20},{14,22},{16,24},... | collective-permute-start | bytes 3145736 | tf_op jit(solution)/shard_map/ppermute | solution.py:316
  13.1 44.4 %collective-permute-start.24 = (bf16[2048,512]{1,0:T(8,128)(2,1)S(1)}, bf16[2048,512]{1,0:T(8,128)(2,1)S(1)}, u32[]{:S(2)}, u32[]{:S(2)}) collective-permute-start(bf16[2048,512]{1,0:T(8,128)(2,1)S(1)} %get-tuple-element.38.refs_0_.refs_4_.refs_21_.refs_1_), channel_id=1, source_target_pairs={{0,2},{2,0},{4,6},{6,4},{8,10},{10,8},{12,14},{14,12},{16,18},{18,... | collective-permute-start | bytes 6291464 | tf_op jit(solution)/shard_map/ppermute | solution.py:316
  20.6 37.4 %collective-permute-start.25 = (bf16[2048,512]{1,0:T(8,128)(2,1)S(1)}, bf16[2048,512]{1,0:T(8,128)(2,1)S(1)}, u32[]{:S(2)}, u32[]{:S(2)}) collective-permute-start(bf16[2048,512]{1,0:T(8,128)(2,1)S(1)} %get-tuple-element.39.refs_1_.refs_5_.refs_21_.refs_0_), channel_id=1, source_target_pairs={{0,2},{2,0},{4,6},{6,4},{8,10},{10,8},{12,14},{14,12},{16,18},{18,... | collective-permute-start | bytes 6291464 | tf_op jit(solution)/shard_map/ppermute | solution.py:316
  29.6 48.6 %collective-permute-start.21 = (bf16[2048,512]{1,0:T(8,128)(2,1)S(1)}, bf16[2048,512]{1,0:T(8,128)(2,1)}, u32[]{:S(2)}, u32[]{:S(2)}) collective-permute-start(bf16[2048,512]{1,0:T(8,128)(2,1)S(1)} %get-tuple-element.38.refs_0_.refs_4_.refs_21_.refs_1_), channel_id=1, source_target_pairs={{1,0},{0,1},{3,2},{2,3},{5,4},{4,5},{7,6},{6,7},{9,8},{8,9},{11,10... | collective-permute-start | bytes 6291464 | tf_op jit(solution)/shard_map/ppermute | solution.py:423
  31.1 89.0 %collective-permute-start.20 = (bf16[2048,512]{1,0:T(8,128)(2,1)S(1)}, bf16[2048,512]{1,0:T(8,128)(2,1)}, u32[]{:S(2)}, u32[]{:S(2)}) collective-permute-start(bf16[2048,512]{1,0:T(8,128)(2,1)S(1)} %get-tuple-element.39.refs_1_.refs_5_.refs_21_.refs_0_), channel_id=1, source_target_pairs={{1,0},{0,1},{3,2},{2,3},{5,4},{4,5},{7,6},{6,7},{9,8},{8,9},{11,10... | collective-permute-start | bytes 6291464 | tf_op jit(solution)/shard_map/ppermute | solution.py:423
  54.5 65.6 %collective-permute-start.11 = (bf16[256,2048]{1,0:T(8,128)(2,1)}, bf16[256,2048]{1,0:T(8,128)(2,1)}, u32[]{:S(2)}, u32[]{:S(2)}) collective-permute-start(bf16[256,2048]{1,0:T(8,128)(2,1)} %collective-permute-done.3.refs_4_), channel_id=1, source_target_pairs={{0,24},{2,26},{4,28},{6,30},{8,0},{10,2},{12,4},{14,6},{16,8},{18,... | collective-permute-start | bytes 3145736 | tf_op jit(solution)/shard_map/ppermute | solution.py:316
  57.5 63.2 %collective-permute-start.9 = (bf16[256,2048]{1,0:T(8,128)(2,1)}, bf16[256,2048]{1,0:T(8,128)(2,1)}, u32[]{:S(2)}, u32[]{:S(2)}) collective-permute-start(bf16[256,2048]{1,0:T(8,128)(2,1)} %collective-permute-done.3.refs_4_), channel_id=1, source_target_pairs={{0,4},{2,6},{4,0},{6,2},{8,12},{10,14},{12,8},{14,10},{16,20},{18,... | collective-permute-start | bytes 3145736 | tf_op jit(solution)/shard_map/ppermute | solution.py:316
  58.0 62.8 %collective-permute-start.7 = (bf16[256,2048]{1,0:T(8,128)(2,1)}, bf16[256,2048]{1,0:T(8,128)(2,1)}, u32[]{:S(2)}, u32[]{:S(2)}) collective-permute-start(bf16[256,2048]{1,0:T(8,128)(2,1)} %collective-permute-done.1.refs_2_), channel_id=1, source_target_pairs={{0,8},{2,10},{4,12},{6,14},{8,16},{10,18},{12,20},{14,22},{16,24},... | collective-permute-start | bytes 3145736 | tf_op jit(solution)/shard_map/ppermute | solution.py:316
  78.2 45.9 %collective-permute-start.4 = (bf16[256,2048]{1,0:T(8,128)(2,1)}, bf16[256,2048]{1,0:T(8,128)(2,1)}, u32[]{:S(2)}, u32[]{:S(2)}) collective-permute-start(bf16[256,2048]{1,0:T(8,128)(2,1)} %collective-permute-done.3.refs_4_), channel_id=1, source_target_pairs={{0,2},{2,0},{4,6},{6,4},{8,10},{10,8},{12,14},{14,12},{16,18},{18,... | collective-permute-start | bytes 3145736 | tf_op jit(solution)/shard_map/ppermute | solution.py:316
  120.7 35.3 %collective-permute-start.22 = (bf16[2048,512]{1,0:T(8,128)(2,1)}, bf16[2048,512]{1,0:T(8,128)(2,1)}, u32[]{:S(2)}, u32[]{:S(2)}) collective-permute-start(bf16[2048,512]{1,0:T(8,128)(2,1)} %collective-permute-done.21.refs_0_.refs_22_.refs_2_.refs_3_), channel_id=1, source_target_pairs={{0,2},{2,0},{4,6},{6,4},{8,10},{10,8},{12,14},{14,12},{16,18},{18,... | collective-permute-start | bytes 6291464 | tf_op jit(solution)/shard_map/ppermute | solution.py:316
  120.8 35.3 %collective-permute-start.23 = (bf16[2048,512]{1,0:T(8,128)(2,1)}, bf16[2048,512]{1,0:T(8,128)(2,1)}, u32[]{:S(2)}, u32[]{:S(2)}) collective-permute-start(bf16[2048,512]{1,0:T(8,128)(2,1)} %collective-permute-done.20.refs_1_.refs_22_.refs_2_.refs_3_), channel_id=1, source_target_pairs={{0,2},{2,0},{4,6},{6,4},{8,10},{10,8},{12,14},{14,12},{16,18},{18,... | collective-permute-start | bytes 6291464 | tf_op jit(solution)/shard_map/ppermute | solution.py:316
  132.9 22.6 %collective-permute-start.13 = (bf16[96,2048]{1,0:T(8,128)(2,1)S(1)}, bf16[96,2048]{1,0:T(8,128)(2,1)S(1)}, u32[]{:S(2)}, u32[]{:S(2)}) collective-permute-start(bf16[96,2048]{1,0:T(8,128)(2,1)S(1)} %slice.22), channel_id=1, source_target_pairs={{0,4},{2,6},{4,0},{6,2},{8,12},{10,14},{12,8},{14,10},{16,20},{18,... | collective-permute-start | bytes 1179656 | tf_op jit(solution)/shard_map/ppermute | solution.py:316
  134.5 20.5 %collective-permute-start.15 = (bf16[80,2048]{1,0:T(8,128)(2,1)S(1)}, bf16[80,2048]{1,0:T(8,128)(2,1)S(1)}, u32[]{:S(2)}, u32[]{:S(2)}) collective-permute-start(bf16[80,2048]{1,0:T(8,128)(2,1)S(1)} %slice.23), channel_id=1, source_target_pairs={{0,8},{2,10},{4,12},{6,14},{8,16},{10,18},{12,20},{14,22},{16,24},... | collective-permute-start | bytes 983048 | tf_op jit(solution)/shard_map/ppermute | solution.py:316
  136.6 18.9 %collective-permute-start.18 = (bf16[80,2048]{1,0:T(8,128)(2,1)S(1)}, bf16[80,2048]{1,0:T(8,128)(2,1)S(1)}, u32[]{:S(2)}, u32[]{:S(2)}) collective-permute-start(bf16[80,2048]{1,0:T(8,128)(2,1)S(1)} %collective-permute-done.17.refs_18_), channel_id=1, source_target_pairs={{0,2},{2,0},{4,6},{6,4},{8,10},{10,8},{12,14},{14,12},{16,18},{18,... | collective-permute-start | bytes 983048 | tf_op jit(solution)/shard_map/ppermute | solution.py:316
  155.0 22.1 %collective-permute-start.10 = (bf16[256,2048]{1,0:T(8,128)(2,1)}, bf16[256,2048]{1,0:T(8,128)(2,1)S(1)}, u32[]{:S(2)}, u32[]{:S(2)}) collective-permute-start(bf16[256,2048]{1,0:T(8,128)(2,1)} %collective-permute-done.9.refs_10_), channel_id=1, source_target_pairs={{0,2},{2,0},{4,6},{6,4},{8,10},{10,8},{12,14},{14,12},{16,18},{18,... | collective-permute-start | bytes 3145736 | tf_op jit(solution)/shard_map/ppermute | solution.py:316
  155.5 23.1 %collective-permute-start.12 = (bf16[256,2048]{1,0:T(8,128)(2,1)}, bf16[256,2048]{1,0:T(8,128)(2,1)}, u32[]{:S(2)}, u32[]{:S(2)}) collective-permute-start(bf16[256,2048]{1,0:T(8,128)(2,1)} %collective-permute-done.11.refs_12_), channel_id=1, source_target_pairs={{0,2},{2,0},{4,6},{6,4},{8,10},{10,8},{12,14},{14,12},{16,18},{18,... | collective-permute-start | bytes 3145736 | tf_op jit(solution)/shard_map/ppermute | solution.py:316
  155.6 24.0 %collective-permute-start.8 = (bf16[256,2048]{1,0:T(8,128)(2,1)}, bf16[256,2048]{1,0:T(8,128)(2,1)}, u32[]{:S(2)}, u32[]{:S(2)}) collective-permute-start(bf16[256,2048]{1,0:T(8,128)(2,1)} %collective-permute-done.7.refs_8_), channel_id=1, source_target_pairs={{0,2},{2,0},{4,6},{6,4},{8,10},{10,8},{12,14},{14,12},{16,18},{18,... | collective-permute-start | bytes 3145736 | tf_op jit(solution)/shard_map/ppermute | solution.py:316
  156.1 20.4 %collective-permute-start.14 = (bf16[96,2048]{1,0:T(8,128)(2,1)S(1)}, bf16[96,2048]{1,0:T(8,128)(2,1)S(1)}, u32[]{:S(2)}, u32[]{:S(2)}) collective-permute-start(bf16[96,2048]{1,0:T(8,128)(2,1)S(1)} %collective-permute-done.13.refs_14_), channel_id=1, source_target_pairs={{0,2},{2,0},{4,6},{6,4},{8,10},{10,8},{12,14},{14,12},{16,18},{18,... | collective-permute-start | bytes 1179656 | tf_op jit(solution)/shard_map/ppermute | solution.py:316
  174.9 39.8 %collective-permute-start.27 = (bf16[256,2048]{1,0:T(8,128)(2,1)}, bf16[256,2048]{1,0:T(8,128)(2,1)S(1)}, u32[]{:S(2)}, u32[]{:S(2)}) collective-permute-start(bf16[256,2048]{1,0:T(8,128)(2,1)} %get-tuple-element.36.refs_10_), channel_id=1, source_target_pairs={{0,4},{2,6},{4,0},{6,2},{8,12},{10,14},{12,8},{14,10},{16,20},{18,... | collective-permute-start | bytes 3145736 | tf_op jit(solution)/shard_map/ppermute | solution.py:316
  176.5 47.1 %collective-permute-start.28 = (bf16[256,2048]{1,0:T(8,128)(2,1)S(1)}, bf16[256,2048]{1,0:T(8,128)(2,1)S(1)}, u32[]{:S(2)}, u32[]{:S(2)}) collective-permute-start(bf16[256,2048]{1,0:T(8,128)(2,1)S(1)} %copy-done.10), channel_id=1, source_target_pairs={{0,4},{2,6},{4,0},{6,2},{8,12},{10,14},{12,8},{14,10},{16,20},{18,... | collective-permute-start | bytes 3145736 | tf_op jit(solution)/shard_map/ppermute | solution.py:316
  177.0 69.1 %collective-permute-start.26 = (bf16[256,2048]{1,0:T(8,128)(2,1)}, bf16[256,2048]{1,0:T(8,128)(2,1)S(1)}, u32[]{:S(2)}, u32[]{:S(2)}) collective-permute-start(bf16[256,2048]{1,0:T(8,128)(2,1)} %get-tuple-element.35.refs_25_), channel_id=1, source_target_pairs={{0,4},{2,6},{4,0},{6,2},{8,12},{10,14},{12,8},{14,10},{16,20},{18,... | collective-permute-start | bytes 3145736 | tf_op jit(solution)/shard_map/ppermute | solution.py:316
  178.6 110.2 %collective-permute-start.31 = (bf16[256,2048]{1,0:T(8,128)(2,1)}, bf16[256,2048]{1,0:T(8,128)(2,1)S(1)}, u32[]{:S(2)}, u32[]{:S(2)}) collective-permute-start(bf16[256,2048]{1,0:T(8,128)(2,1)} %get-tuple-element.34.refs_26_), channel_id=1, source_target_pairs={{0,4},{2,6},{4,0},{6,2},{8,12},{10,14},{12,8},{14,10},{16,20},{18,... | collective-permute-start | bytes 3145736 | tf_op jit(solution)/shard_map/ppermute | solution.py:316
  250.6 38.1 %collective-permute-start.32 = (bf16[256,2048]{1,0:T(8,128)(2,1)}, bf16[256,2048]{1,0:T(8,128)(2,1)S(1)}, u32[]{:S(2)}, u32[]{:S(2)}) collective-permute-start(bf16[256,2048]{1,0:T(8,128)(2,1)} %get-tuple-element.33.refs_27_), channel_id=1, source_target_pairs={{0,8},{2,10},{4,12},{6,14},{1,9},{3,11},{5,13},{7,15}} | collective-permute-start | bytes 3145736 | tf_op jit(solution)/shard_map/ppermute | solution.py:324
  252.0 38.7 %collective-permute-start.33 = (bf16[256,2048]{1,0:T(8,128)(2,1)}, bf16[256,2048]{1,0:T(8,128)(2,1)}, u32[]{:S(2)}, u32[]{:S(2)}) collective-permute-start(bf16[256,2048]{1,0:T(8,128)(2,1)} %get-tuple-element.32.refs_28_), channel_id=1, source_target_pairs={{24,16},{26,18},{28,20},{30,22},{25,17},{27,19},{29,21},{31,23}} | collective-permute-start | bytes 3145736 | tf_op jit(solution)/shard_map/ppermute | solution.py:324
  295.2 23.1 %collective-permute-start.35 = (bf16[256,2048]{1,0:T(8,128)(2,1)S(1)}, bf16[256,2048]{1,0:T(8,128)(2,1)}, u32[]{:S(2)}, u32[]{:S(2)}) collective-permute-start(bf16[256,2048]{1,0:T(8,128)(2,1)S(1)} %get-tuple-element.30.refs_2_.refs_5_.refs_6_), channel_id=1, source_target_pairs={{16,8},{18,10},{20,12},{22,14},{24,16},{26,18},{28,20},{30,22},{17... | collective-permute-start | bytes 3145736 | tf_op jit(solution)/shard_map/ppermute | solution.py:324
  296.9 48.8 %collective-permute-start.30 = (bf16[2048,512]{1,0:T(8,128)(2,1)}, bf16[2048,512]{1,0:T(8,128)(2,1)}, u32[]{:S(2)}, u32[]{:S(2)}) collective-permute-start(bf16[2048,512]{1,0:T(8,128)(2,1)} %get-tuple-element.22), channel_id=1, source_target_pairs={{0,1},{1,0},{2,3},{3,2},{4,5},{5,4},{6,7},{7,6},{8,9},{9,8},{10,11... | collective-permute-start | bytes 6291464 | tf_op jit(solution)/shard_map/ppermute | solution.py:426
  298.4 89.6 %collective-permute-start.29 = (bf16[2048,512]{1,0:T(8,128)(2,1)}, bf16[2048,512]{1,0:T(8,128)(2,1)}, u32[]{:S(2)}, u32[]{:S(2)}) collective-permute-start(bf16[2048,512]{1,0:T(8,128)(2,1)} %get-tuple-element.21), channel_id=1, source_target_pairs={{0,1},{1,0},{2,3},{3,2},{4,5},{5,4},{6,7},{7,6},{8,9},{9,8},{10,11... | collective-permute-start | bytes 6291464 | tf_op jit(solution)/shard_map/ppermute | solution.py:426
  298.9 22.2 %collective-permute-start.34 = (bf16[256,2048]{1,0:T(8,128)(2,1)S(1)}, bf16[256,2048]{1,0:T(8,128)(2,1)}, u32[]{:S(2)}, u32[]{:S(2)}) collective-permute-start(bf16[256,2048]{1,0:T(8,128)(2,1)S(1)} %get-tuple-element.31.refs_1_.refs_4_.refs_5_), channel_id=1, source_target_pairs={{0,8},{2,10},{4,12},{6,14},{8,16},{10,18},{12,20},{14,22},{1,9},{3... | collective-permute-start | bytes 3145736 | tf_op jit(solution)/shard_map/ppermute | solution.py:324
  319.8 74.3 %collective-permute-start.37 = (bf16[256,2048]{1,0:T(8,128)(2,1)S(1)}, bf16[256,2048]{1,0:T(8,128)(2,1)S(1)}, u32[]{:S(2)}, u32[]{:S(2)}) collective-permute-start(bf16[256,2048]{1,0:T(8,128)(2,1)S(1)} %add_convert_fusion.refs_3_), channel_id=1, source_target_pairs={{8,0},{10,2},{12,4},{14,6},{16,8},{18,10},{20,12},{22,14},{24,16},... | collective-permute-start | bytes 3145736 | tf_op jit(solution)/shard_map/ppermute | solution.py:324
  322.7 71.5 %collective-permute-start.36 = (bf16[256,2048]{1,0:T(8,128)(2,1)S(1)}, bf16[256,2048]{1,0:T(8,128)(2,1)}, u32[]{:S(2)}, u32[]{:S(2)}) collective-permute-start(bf16[256,2048]{1,0:T(8,128)(2,1)S(1)} %add_convert_fusion.1.refs_2_), channel_id=1, source_target_pairs={{0,8},{2,10},{4,12},{6,14},{8,16},{10,18},{12,20},{14,22},{16,24},... | collective-permute-start | bytes 3145736 | tf_op jit(solution)/shard_map/ppermute | solution.py:324
  (31 other events, 887.6 us)
